TPU v7x, 256 devices: a 8x8x2 block of a 8x8x16 slice. The times are simulated.
256 devices in a mesh: groups: 2 (over z), dap: 128 (over x, y, core).
Axes of the slice: x: 8, y: 8, z: 2, core: 2. Of those that a mesh axis runs over, the one named last changes fastest.
The devices are a block of a 8x8x16 slice.
Arguments:
- homolog_tensor: bfloat16 [1024, 256, 256], P(('groups', 'dap')), parts along dimension 0, may hold values from -1 to 1
- couple_tensor: bfloat16 [512, 256, 128], P(('groups', 'dap')), parts along dimension 0, may hold values from -6 to 6
- horizontal_drop_filter: int32 [512, 256], P('groups'), parts along dimension 0, may hold values 0 or 1
- couple_offset_matrix: bfloat16 [128, 8], replicated, may hold values from -0.29882812 to 0.29882812
- horizontal_attend_matrix: bfloat16 [256, 1024], replicated, may hold values from -0.375 to 0.375
- horizontal_exit_matrix: bfloat16 [256, 256], replicated, may hold values from -0.375 to 0.375
- vertical_attend_matrix: bfloat16 [256, 1024], replicated, may hold values from -0.375 to 0.375
- vertical_exit_matrix: bfloat16 [256, 256], replicated, may hold values from -0.375 to 0.375
- averaged_product_flanks: bfloat16 [256, 64], replicated, may hold values from -0.375 to 0.375
- averaged_product_exit: bfloat16 [1024, 128], replicated, may hold values from -1 to 1
Outputs:
- alignment_output: bfloat16 [1024, 256, 256], P('groups', 'dap'), parts along dimension 0
- pair_output_state: bfloat16 [512, 256, 128], P(('groups', 'dap')), parts along dimension 0
There are 2 independent parts, one for each index of `groups`. A program takes and returns all parts, laid end to end along the dimension named above; an argument that names none is the same for every part. Nothing has to cross between parts.
All inputs are finite; a program needn't handle non-finite values.
Results may differ from a plain program's by a relative error of at most 0.012.
Values may be sent and summed in bfloat16 or wider, within the bound.
A program may use at most 64 MiB of HBM per device.

v0:
```python
import jax
import jax.numpy as jnp
from jax import lax
from jax.sharding import Mesh
from jax.sharding import PartitionSpec as P

HEAD_NUMBER = 8
HEAD_WIDTH = 32
FACTOR_FEATURES = 32
DAP = ("dap_0", "dap_1", "dap_2")
GROUPS_DAP = ("groups", "dap_0", "dap_1", "dap_2")


def joined_along(tiles, dim):
    tiles = jnp.moveaxis(tiles, 0, dim)
    dims = tiles.shape
    return tiles.reshape(*dims[:dim], dims[dim] * dims[dim + 1], *dims[dim + 2 :])


def stacked_from(shard, axes, order):
    tiles = shard[None]
    for k in order:
        tiles = lax.all_gather(tiles, axes[k], axis=0, tiled=True)
    carried = [lax.axis_size(axes[k]) for k in reversed(order)]
    tiles = tiles.reshape(*carried, *shard.shape)
    turned = sorted(range(len(order)), key=lambda place: order[len(order) - 1 - place])
    return tiles.transpose(*turned, *range(len(order), tiles.ndim)).reshape(-1, *shard.shape)


def gather_axes(shard, axes, order, dim):
    return joined_along(stacked_from(shard, axes, order), dim)


def standardise_features(values):
    values = values.astype(jnp.float32)
    center = values - jnp.mean(values, axis=-1, keepdims=True)
    spread = jnp.mean(center * center, axis=-1, keepdims=True)
    return center * lax.rsqrt(spread + 1e-05)


def attend(normed, w_qkvg, w_out, bias):
    batch, length = (normed.shape[0], normed.shape[1])
    proj = jnp.einsum("blc,cf->blf", normed, w_qkvg, preferred_element_type=jnp.float32)
    proj = proj.reshape(batch, length, 4, HEAD_NUMBER, HEAD_WIDTH)
    query = (proj[:, :, 0] * HEAD_WIDTH ** (-0.5)).astype(jnp.bfloat16)
    keys = proj[:, :, 1].astype(jnp.bfloat16)
    values = proj[:, :, 2].astype(jnp.bfloat16)
    gate = proj[:, :, 3]
    if bias is None:
        bias = jnp.zeros((HEAD_NUMBER, length, length), jnp.bfloat16)

    def one_head(items):
        qh, kh, vh, bh = items
        scores = jnp.einsum("bid,bjd->bij", qh, kh, preferred_element_type=jnp.float32)
        scores = scores + bh.astype(jnp.float32)[None]
        weights = jax.nn.softmax(scores, axis=-1).astype(jnp.bfloat16)
        return jnp.einsum("bij,bjd->bid", weights, vh, preferred_element_type=jnp.float32)

    heads = lax.map(
        one_head,
        (jnp.moveaxis(query, 2, 0), jnp.moveaxis(keys, 2, 0), jnp.moveaxis(values, 2, 0), bias),
    )
    heads = jnp.moveaxis(heads, 0, 2)
    gated = (
        (jax.nn.sigmoid(gate) * heads)
        .astype(jnp.bfloat16)
        .reshape(batch, length, HEAD_NUMBER * HEAD_WIDTH)
    )
    return jnp.einsum("blk,kc->blc", gated, w_out, preferred_element_type=jnp.float32)


def shards(
    homolog_tensor,
    couple_tensor,
    horizontal_drop_filter,
    couple_offset_matrix,
    horizontal_attend_matrix,
    horizontal_exit_matrix,
    vertical_attend_matrix,
    vertical_exit_matrix,
    averaged_product_flanks,
    averaged_product_exit,
):
    normed_pair = standardise_features(couple_tensor).astype(jnp.bfloat16)
    own_bias = jnp.einsum(
        "ijz,zh->hij", normed_pair, couple_offset_matrix, preferred_element_type=jnp.float32
    ).astype(jnp.bfloat16)
    bias = gather_axes(own_bias, DAP, (0, 1, 2), 1)
    starting_answer = standardise_features(homolog_tensor).astype(jnp.bfloat16)
    perform_refresh = attend(
        starting_answer, horizontal_attend_matrix, horizontal_exit_matrix, bias
    )
    homolog_later = (
        homolog_tensor.astype(jnp.float32)
        + horizontal_drop_filter.astype(jnp.float32) * (1.0 / 0.9) * perform_refresh
    ).astype(jnp.bfloat16)
    incoming_blocks = lax.all_to_all(homolog_later, DAP, split_axis=1, concat_axis=0, tiled=True)
    column_layout = jnp.swapaxes(incoming_blocks, 0, 1)
    perform_refresh = attend(
        standardise_features(column_layout).astype(jnp.bfloat16),
        vertical_attend_matrix,
        vertical_exit_matrix,
        None,
    )
    alignment_output = jnp.swapaxes(
        (column_layout.astype(jnp.float32) + perform_refresh).astype(jnp.bfloat16), 0, 1
    )
    final_result = standardise_features(alignment_output).astype(jnp.bfloat16)
    factors = jnp.einsum(
        "sic,cf->sif", final_result, averaged_product_flanks, preferred_element_type=jnp.float32
    )
    left = factors[..., :FACTOR_FEATURES].astype(jnp.bfloat16)
    right = factors[..., FACTOR_FEATURES:].astype(jnp.bfloat16)
    total = left.shape[0]
    own_rows = left.shape[1]
    piece = lax.all_gather(right, DAP, axis=1, tiled=True)
    outer = jnp.einsum("sic,sjd->ijcd", left, piece, preferred_element_type=jnp.float32) / total
    outer = outer.astype(jnp.bfloat16).reshape(
        own_rows, piece.shape[1], FACTOR_FEATURES * FACTOR_FEATURES
    )
    change = jnp.einsum(
        "ijk,kz->ijz", outer, averaged_product_exit, preferred_element_type=jnp.float32
    )
    pair_output_state = (couple_tensor.astype(jnp.float32) + change).astype(jnp.bfloat16)
    return (alignment_output, pair_output_state)


def solution(mesh):
    torus = Mesh(
        mesh.devices.reshape(mesh.shape["groups"], 8, 8, 2), ("groups", "dap_0", "dap_1", "dap_2")
    )
    return jax.shard_map(
        shards,
        mesh=torus,
        in_specs=(
            P(GROUPS_DAP, None, None),
            P(GROUPS_DAP, None, None),
            P("groups", None),
            P(),
            P(),
            P(),
            P(),
            P(),
            P(),
            P(),
        ),
        out_specs=(P("groups", DAP, None), P(GROUPS_DAP, None, None)),
        check_vma=False,
    )
```

profile of v0, /device:TPU:513, one launch (start us, length us, event | category | flops | bytes accessed | tf_op | source)
XLA Modules:
  0.0 365.0 jit_solution(12928804633516290471)
XLA Ops:
  9.5 1.2 fusion.37
  10.7 20.9 %all-gather = bf16[64,2,256]{2,0,1:T(8,128)(2,1)S(1)} all-gather(bf16[8,2,256]{2,0,1:T(8,128)(2,1)S(1)} %fusion.37), channel_id=2, replica_groups=mesh['groups'=2,'dap_0'=8,'dap_1'=8,'dap_2'=2] {'dap_0'}, dimensions={0}, use_global_device_ids=true | all-gather | bytes 73728 | tf_op jit(solution)/shard_map/all_gather | solution.py:23
  31.7 30.9 %all_gather.13 = bf16[64,8,2,256]{3,1,0,2:T(8,128)(2,1)} all-gather(bf16[8,8,2,256]{3,1,0,2:T(8,128)(2,1)S(1)} %bitcast.194), channel_id=1, replica_groups=mesh['groups'=2,'dap_0'=8,'dap_1'=8,'dap_2'=2] {'dap_1'}, dimensions={0}, use_global_device_ids=true | all-gather | bytes 589824 | tf_op jit(solution)/shard_map/all_gather | solution.py:23
  62.6 1.3 convert_reduce_fusion
  63.9 1.4 fusion.38
  65.3 2.0 fusion.59
  71.5 27.3 %all-gather.4.cloned.1.call-done = bf16[128,8,2,256]{3,1,0,2:T(8,128)(2,1)} async-done(((bf16[64,8,2,256]{3,1,0,2:T(8,128)(2,1)}), bf16[128,8,2,256]{3,1,0,2:T(8,128)(2,1)}) %all-gather.4.cloned.1.call-update) | async-done | bytes 1048592 | tf_op jit(solution)/shard_map/all_gather | solution.py:23
  98.8 1.4 copy.52
  101.0 36.0 %while.20 = (s32[]{:T(128)}, f32[8,4,256,32]{2,3,0,1:T(8,128)}, bf16[8,4,256,32]{2,3,0,1:T(8,128)(2,1)}, bf16[8,4,256,32]{2,3,0,1:T(8,128)(2,1)}, bf16[8,256,256...) while((s32[]{:T(128)}, f32[8,4,256,32]{2,3,0,1:T(8,128)}, ...), condition=%wide.region_7.8_spmd, body=%wide.region_4.7_spmd.sunk | while | flops 52233728 | bytes 4533337 | solution.py:59
  101.0 1.4 fusion.104
  102.4 1.2 convolution_add_fusion.3
  103.7 1.9 fusion.105
  105.6 1.4 fusion.104
  106.9 1.2 convolution_add_fusion.3
  108.2 1.9 fusion.105
  110.0 1.4 fusion.104
  111.4 1.2 convolution_add_fusion.3
  112.6 1.9 fusion.105
  114.5 1.4 fusion.104
  115.9 1.2 convolution_add_fusion.3
  117.1 1.8 fusion.105
  119.0 1.4 fusion.104
  120.4 1.2 convolution_add_fusion.3
  121.6 1.8 fusion.105
  123.5 1.4 fusion.104
  124.9 1.2 convolution_add_fusion.3
  126.1 1.8 fusion.105
  128.0 1.4 fusion.104
  129.3 1.2 convolution_add_fusion.3
  130.6 1.8 fusion.105
  132.4 1.4 fusion.104
  133.8 1.2 convolution_add_fusion.3
  135.1 1.9 fusion.105
  136.9 1.8 fusion.54
  138.8 1.3 fusion.31
  140.1 1.2 copy.59
  141.3 14.5 %all-to-all-start = ((bf16[4,256,256]{2,0,1:T(4,128)(2,1)}), bf16[4,256,256]{2,0,1:T(4,128)(2,1)S(1)}, u32[]{:S(2)}, u32[]{:S(2)}) async-start(bf16[4,256,256]{2,0,1:T(4,128)(2,1)} %copy.59), calls=%async_computation | async-start | bytes 1048576 | tf_op jit(solution)/shard_map/all_to_all | solution.py:97
  156.1 18.9 %all-to-all-done = bf16[4,256,256]{2,0,1:T(4,128)(2,1)S(1)} async-done(((bf16[4,256,256]{2,0,1:T(4,128)(2,1)}), bf16[4,256,256]{2,0,1:T(4,128)(2,1)S(1)}, u32[]{:S(2)}, u32[]{:S(2)}) %all-to-all-start) | async-done | bytes 524320 | tf_op jit(solution)/shard_map/all_to_all | solution.py:97
  176.0 1.6 multiply_reduce_fusion
  177.6 1.8 multiply_convert_fusion.1
  180.3 1.8 copy-done.1
  182.1 1.7 convert.21
  184.5 2.1 slice_bitcast_fusion
  186.6 73.0 %while.21 = (s32[]{:T(128)}, f32[8,2,512,32]{2,3,0,1:T(8,128)}, bf16[8,2,512,32]{2,3,0,1:T(8,128)(2,1)S(1)}, bf16[8,2,512,32]{2,3,0,1:T(8,128)(2,1)}, bf16[8,2,512,32]{2,3,0,1:T(8,128)(2,1)S(1)}, /*index=5*/s32[]{:T(128)}) while((s32[]{:T(128)}, f32[8,2,512,32]{2,3,0,1:T(8,128)}, bf16[8,2,512,32]{2,3,0,1:T(8,128)(2,1)S(1)}, ...), condition=%wide.region_13.14_spmd, body=%wide.region_10.13_spmd.sunk | while | flops 67108864 | bytes 1507417 | solution.py:59
  190.1 3.8 %dot_general.47 = f32[2,512,32]{2,1,0:T(8,128)} custom-call(bf16[2,512,32]{2,1,0:T(8,128)(2,1)} %bitcast.177, bf16[2,512,32]{2,1,0:T(8,128)(2,1)} %bitcast.176, bf16[2,512,32]{2,1,0:T(8,128)(2,1)} %bitcast.178), custom_call_target="tpu_custom_call" | custom-call | flops 67108864 | bytes 196608 | tf_op jit(solution)/shard_map/while/body/eval_jaxpr/bij,bjd->bid/dot_general | solution.py:57
  193.9 1.2 copy.111
  199.2 3.8 %dot_general.47 = f32[2,512,32]{2,1,0:T(8,128)} custom-call(bf16[2,512,32]{2,1,0:T(8,128)(2,1)} %bitcast.177, bf16[2,512,32]{2,1,0:T(8,128)(2,1)} %bitcast.176, bf16[2,512,32]{2,1,0:T(8,128)(2,1)} %bitcast.178), custom_call_target="tpu_custom_call" | custom-call | flops 67108864 | bytes 196608 | tf_op jit(solution)/shard_map/while/body/eval_jaxpr/bij,bjd->bid/dot_general | solution.py:57
  203.0 1.2 copy.111
  208.3 3.8 %dot_general.47 = f32[2,512,32]{2,1,0:T(8,128)} custom-call(bf16[2,512,32]{2,1,0:T(8,128)(2,1)} %bitcast.177, bf16[2,512,32]{2,1,0:T(8,128)(2,1)} %bitcast.176, bf16[2,512,32]{2,1,0:T(8,128)(2,1)} %bitcast.178), custom_call_target="tpu_custom_call" | custom-call | flops 67108864 | bytes 196608 | tf_op jit(solution)/shard_map/while/body/eval_jaxpr/bij,bjd->bid/dot_general | solution.py:57
  212.2 1.2 copy.111
  217.4 3.8 %dot_general.47 = f32[2,512,32]{2,1,0:T(8,128)} custom-call(bf16[2,512,32]{2,1,0:T(8,128)(2,1)} %bitcast.177, bf16[2,512,32]{2,1,0:T(8,128)(2,1)} %bitcast.176, bf16[2,512,32]{2,1,0:T(8,128)(2,1)} %bitcast.178), custom_call_target="tpu_custom_call" | custom-call | flops 67108864 | bytes 196608 | tf_op jit(solution)/shard_map/while/body/eval_jaxpr/bij,bjd->bid/dot_general | solution.py:57
  221.3 1.2 copy.111
  226.6 3.8 %dot_general.47 = f32[2,512,32]{2,1,0:T(8,128)} custom-call(bf16[2,512,32]{2,1,0:T(8,128)(2,1)} %bitcast.177, bf16[2,512,32]{2,1,0:T(8,128)(2,1)} %bitcast.176, bf16[2,512,32]{2,1,0:T(8,128)(2,1)} %bitcast.178), custom_call_target="tpu_custom_call" | custom-call | flops 67108864 | bytes 196608 | tf_op jit(solution)/shard_map/while/body/eval_jaxpr/bij,bjd->bid/dot_general | solution.py:57
  230.4 1.2 copy.111
  235.7 3.8 %dot_general.47 = f32[2,512,32]{2,1,0:T(8,128)} custom-call(bf16[2,512,32]{2,1,0:T(8,128)(2,1)} %bitcast.177, bf16[2,512,32]{2,1,0:T(8,128)(2,1)} %bitcast.176, bf16[2,512,32]{2,1,0:T(8,128)(2,1)} %bitcast.178), custom_call_target="tpu_custom_call" | custom-call | flops 67108864 | bytes 196608 | tf_op jit(solution)/shard_map/while/body/eval_jaxpr/bij,bjd->bid/dot_general | solution.py:57
  239.5 1.2 copy.111
  244.8 3.8 %dot_general.47 = f32[2,512,32]{2,1,0:T(8,128)} custom-call(bf16[2,512,32]{2,1,0:T(8,128)(2,1)} %bitcast.177, bf16[2,512,32]{2,1,0:T(8,128)(2,1)} %bitcast.176, bf16[2,512,32]{2,1,0:T(8,128)(2,1)} %bitcast.178), custom_call_target="tpu_custom_call" | custom-call | flops 67108864 | bytes 196608 | tf_op jit(solution)/shard_map/while/body/eval_jaxpr/bij,bjd->bid/dot_general | solution.py:57
  248.6 1.2 copy.111
  253.9 3.8 %dot_general.47 = f32[2,512,32]{2,1,0:T(8,128)} custom-call(bf16[2,512,32]{2,1,0:T(8,128)(2,1)} %bitcast.177, bf16[2,512,32]{2,1,0:T(8,128)(2,1)} %bitcast.176, bf16[2,512,32]{2,1,0:T(8,128)(2,1)} %bitcast.178), custom_call_target="tpu_custom_call" | custom-call | flops 67108864 | bytes 196608 | tf_op jit(solution)/shard_map/while/body/eval_jaxpr/bij,bjd->bid/dot_general | solution.py:57
  257.8 1.2 copy.111
  259.7 1.8 fusion.55
  264.1 77.3 %all-gather.6.cloned.1.call-done = bf16[512,256,32]{0,2,1:T(8,128)(2,1)} async-done(((bf16[512,2,32]{0,2,1:T(8,128)(2,1)}), bf16[512,256,32]{0,2,1:T(8,128)(2,1)}) %all-gather.6.cloned.1.call-update) | async-done | bytes 8388624 | tf_op jit(solution)/shard_map/all_gather | solution.py:116
  341.4 9.4 %fusion.26 = bf16[2,256,32,32]{2,3,0,1:T(8,128)(2,1)} fusion(bf16[512,256,32]{0,2,1:T(8,128)(2,1)} %all-gather.6.cloned.1.call-done, bf16[512,2,64]{0,2,1:T(8,128)(2,1)S(1)} %convolution_convert_fusion), kind=kOutput, calls=%fused_computation.30 | convolution fusion | flops 537919488 | bytes 9502720 | tf_op jit(solution)/shard_map/sic,sjd->ijcd/dot_general | solution.py:117
  350.8 6.2 %copy.71 = bf16[2,256,32,32]{1,3,2,0:T(8,128)(2,1)S(1)} copy(bf16[2,256,32,32]{2,3,0,1:T(8,128)(2,1)} %fusion.26) | data formatting | bytes 2097152 | tf_op jit(solution)/shard_map/convert_element_type | solution.py:118
  (109 shorter events, 46.8 us)
Async XLA Ops:
  7.2 58.2 %copy-start = (bf16[256,1024]{1,0:T(8,128)(2,1)S(1)}, bf16[256,1024]{1,0:T(8,128)(2,1)}, u32[]{:S(2)}) copy-start(bf16[256,1024]{1,0:T(8,128)(2,1)} %param.18) | copy-start | bytes 1572868
  7.2 91.6 %all-gather.4.cloned.1.call-start = ((), (), s32[]{:S(2)}) async-start(), calls=%async_computation.1 | async-start | bytes 1572864 | tf_op jit(solution)/shard_map/all_gather | solution.py:23
  67.4 3.0 copy-start.2
  67.4 1.1 copy-start.6
  100.9 37.8 %copy-start.3 = (bf16[4,256,256]{2,1,0:T(8,128)(2,1)S(1)}, bf16[4,256,256]{2,1,0:T(8,128)(2,1)}, u32[]{:S(2)}) copy-start(bf16[4,256,256]{2,1,0:T(8,128)(2,1)} %param.14) | copy-start | bytes 1572868
  101.0 37.8 %copy-start.9 = (bf16[256,256]{1,0:T(8,128)(2,1)S(1)}, bf16[256,256]{1,0:T(8,128)(2,1)}, u32[]{:S(2)}) copy-start(bf16[256,256]{1,0:T(8,128)(2,1)} %param.19) | copy-start | bytes 393220
  141.3 38.1 %copy-start.5 = (bf16[256,1024]{1,0:T(8,128)(2,1)S(1)}, bf16[256,1024]{1,0:T(8,128)(2,1)}, u32[]{:S(2)}) copy-start(bf16[256,1024]{1,0:T(8,128)(2,1)} %param.20) | copy-start | bytes 1572868
  141.3 33.6 %all-to-all-start = ((bf16[4,256,256]{2,0,1:T(4,128)(2,1)}), bf16[4,256,256]{2,0,1:T(4,128)(2,1)S(1)}, u32[]{:S(2)}, u32[]{:S(2)}) async-start(bf16[4,256,256]{2,0,1:T(4,128)(2,1)} %copy.59), calls=%async_computation | async-start | bytes 1048576 | tf_op jit(solution)/shard_map/all_to_all | solution.py:97
  155.8 185.6 %all-gather.6.cloned.1.call-start = ((), (), s32[]{:S(2)}) async-start(), calls=%async_computation.2 | async-start | bytes 8454144 | tf_op jit(solution)/shard_map/all_gather | solution.py:116
  180.1 1.9 copy-start.1
  186.6 74.9 %copy-start.8 = (bf16[256,256]{1,0:T(8,128)(2,1)S(1)}, bf16[256,256]{1,0:T(8,128)(2,1)}, u32[]{:S(2)}) copy-start(bf16[256,256]{1,0:T(8,128)(2,1)} %param.21) | copy-start | bytes 393220
  259.7 2.4 copy-start.10
  350.8 6.2 %copy-start.4 = (bf16[2,256,128]{2,1,0:T(8,128)(2,1)S(1)}, bf16[2,256,128]{2,1,0:T(8,128)(2,1)}, u32[]{:S(2)}) copy-start(bf16[2,256,128]{2,1,0:T(8,128)(2,1)} %param.15) | copy-start | bytes 393220
  350.8 6.2 %copy-start.7 = (bf16[1024,128]{1,0:T(8,128)(2,1)S(1)}, bf16[1024,128]{1,0:T(8,128)(2,1)}, u32[]{:S(2)}) copy-start(bf16[1024,128]{1,0:T(8,128)(2,1)} %param.23) | copy-start | bytes 786436
Sparse Core Ops, SparseCore 0:
  62.7 36.0 all-gather.3
  263.1 78.1 all-gather.5
where the time goes:
time: 368 us; the launch traced here: 365 us
  waiting for transfers between devices  124 us (34%)
  local copies, waits for them, and re-layouts  60.6 us (16%)
  matrix products  52.1 us (14%)
  blocking collectives  51.8 us (14%)
  Pallas kernels  30.7 us (8%)
  other arithmetic  16.8 us (5%)
  starting transfers between devices  14.8 us (4%)
  between operations  14.4 us (4%)
    all_gather x1, waiting for transfers between devices, shards(): piece = lax.all_gather(right, DAP, axis=1, tiled=True)  77.3 us
    all_gather x2, blocking collectives, stacked_from(): tiles = lax.all_gather(tiles, axes[k], axis=0, tiled=True)  51.8 us
    dot_general x8, Pallas kernels, one_head(): jnp.einsum('bij,bjd->bid', weights, vh, preferred_element_type=jnp.float32)  30.7 us
    all_gather x1, waiting for transfers between devices, stacked_from(): tiles = lax.all_gather(tiles, axes[k], axis=0, tiled=True)  27.3 us
    dynamic_slice x40, local copies, waits for them, and re-layouts, attend(): lax.map(one_head, (jnp.moveaxis(query, 2, 0), jnp.moveaxis(keys, 2, 0), j...  27.3 us
    all_to_all x1, waiting for transfers between devices, shards(): lax.all_to_all(homolog_later, DAP, split_axis=1, concat_axis=0, tiled=True)  18.9 us
    dynamic_update_slice x16, local copies, waits for them, and re-layouts, attend(): lax.map(one_head, (jnp.moveaxis(query, 2, 0), jnp.moveaxis(keys, 2, 0), j...  15 us
    dot_general x8, matrix products, one_head(): jnp.einsum('bij,bjd->bid', weights, vh, preferred_element_type=jnp.float32)  14.8 us
  transfers between devices with their start and end apart: 3, of which 3 were waited for; matrix products, arithmetic and copies ran while one was open for 2% of the time, Pallas kernels for 0%

commit v1 on v0

v1 whole, which is shorter than its diff:
```python
import jax
import jax.numpy as jnp
from jax import lax
from jax.experimental import pallas as pl
from jax.experimental.pallas import tpu as pltpu
from jax.sharding import Mesh
from jax.sharding import PartitionSpec as P

HEADS = 8
WIDTH = 32
FACTORS = 32
NX, NY, NC = 8, 8, 2
LANES = 128
GROUPS_DAP = ("groups", "dap_0", "dap_1", "dap_2")
DAP = ("dap_0", "dap_1", "dap_2")
MESH = pl.DeviceIdType.MESH
F32, BF16 = jnp.float32, jnp.bfloat16
VMEM = pl.BlockSpec(memory_space=pltpu.VMEM)
LIMIT = 60 * 1024 * 1024
RING_ORDER = (4, 3, 5, 2, 6, 1, 7)


def norm(v):
    center = v - jnp.mean(v, axis=-1, keepdims=True)
    spread = jnp.mean(center * center, axis=-1, keepdims=True)
    return center * lax.rsqrt(spread + 1e-05)


def nt(a, b):
    return lax.dot_general(a, b, (((1,), (1,)), ((), ())), preferred_element_type=F32)


def nn(a, b):
    return jnp.dot(a, b, preferred_element_type=F32)


def here():
    return lax.axis_index("dap_0"), lax.axis_index("dap_1"), lax.axis_index("dap_2")


def place(x, y, c):
    return {"dap_0": x, "dap_1": y, "dap_2": c}


def greet(peers):
    sem = pltpu.get_barrier_semaphore()
    for peer in peers:
        pl.semaphore_signal(sem, inc=1, device_id=peer, device_id_type=MESH)
    pl.semaphore_wait(sem, len(peers))


def x_peers(x, y, c):
    return [place((x + k) % NX, y, c) for k in RING_ORDER]


def y_peers(x, y, c):
    return [place(x, (y + k) % NY, c) for k in RING_ORDER]


def push(src, dst, send, recv, peer):
    copy = pltpu.make_async_remote_copy(
        src_ref=src, dst_ref=dst, send_sem=send, recv_sem=recv, device_id=peer, device_id_type=MESH
    )
    copy.start()
    return copy


def keep(src, dst, sem):
    copy = pltpu.make_async_copy(src, dst, sem)
    copy.start()
    return copy


def wide_y(x, y, c):
    out = [(NY * NC - 2, place(x, y, 1 - c), y, 1 - c)]
    for k in RING_ORDER:
        for f in range(NC):
            cc = (c + f) % NC
            yy = (y + k) % NY
            out.append((2 * (k - 1) + f, place(x, yy, cc), yy, cc))
    return out


def wide_x(x, y, c):
    out = [(NX * NC - 2, place(x, y, 1 - c), x, 1 - c)]
    for k in RING_ORDER:
        for f in range(NC):
            cc = (c + f) % NC
            xx = (x + k) % NX
            out.append((2 * (k - 1) + f, place(xx, y, cc), xx, cc))
    return out


def bias_rows_kernel(pair_ref, w_ref, out_ref):
    zn = norm(pair_ref[...].astype(F32)).astype(BF16)
    rows = nt(w_ref[...], zn)
    length = rows.shape[1] // 2
    both = jnp.concatenate([rows[:, :length], rows[:, length:]], axis=0).astype(BF16)
    for k in range(2):
        out_ref[k] = both[:, k * LANES : (k + 1) * LANES]


def bias_gather_kernel(
    own, full, keep_sem, s0, r0, s1, r1, s2, r2, s3, r3, s4, r4, s5, r5
):
    x, y, c = here()
    yc = y * NC + c
    mine = [keep(own.at[k], full.at[k, x, yc], keep_sem.at[k]) for k in range(2)]
    wy, wx = wide_y(x, y, c), wide_x(x, y, c)
    greet([p for _, p, _, _ in wy] + [p for _, p, _, _ in wx[1:]])
    first0 = [push(own.at[0], full.at[0, x, yc], s0.at[n], r0.at[n], p) for n, p, _, _ in wy]
    first1 = [push(own.at[1], full.at[1, x, yc], s1.at[n], r1.at[n], p) for n, p, _, _ in wx]
    for m in mine:
        m.wait()
    for m in first0:
        m.wait_recv()
    half = pl.ds(c * NY, NY)
    second0 = [
        push(full.at[0, x, half], full.at[0, x, half], s2.at[k - 1], r2.at[k - 1], place((x + k) % NX, y, c))
        for k in RING_ORDER
    ]
    for m in first1:
        m.wait_recv()
    halfx, pair = pl.ds(c * (NX // 2), NX // 2), pl.ds(y * NC, NC)
    second1 = [
        push(full.at[1, halfx, pair], full.at[1, halfx, pair], s3.at[k - 1], r3.at[k - 1], place(x, (y + k) % NY, c))
        for k in RING_ORDER
    ]
    other = place(x, y, 1 - c)
    third = []
    for n in reversed(range(NX - 1)):
        k = RING_ORDER[n]
        second0[n].wait_recv()
        xs = (x + NX - k) % NX
        third.append(push(full.at[0, xs, half], full.at[0, xs, half], s4.at[k - 1], r4.at[k - 1], other))
        second1[n].wait_recv()
        pairs = pl.ds(((y + NY - k) % NY) * NC, NC)
        third.append(push(full.at[1, halfx, pairs], full.at[1, halfx, pairs], s5.at[k - 1], r5.at[k - 1], other))
    for m in third:
        m.wait_recv()
    for m in first0 + first1 + second0 + second1 + third:
        m.wait_send()


def heads_of(q_ref, k_ref, v_ref, rows, bias_of):
    length = k_ref.shape[0]
    lane = lax.broadcasted_iota(jnp.int32, (1, LANES), 1) // WIDTH
    per = LANES // WIDTH
    out = []
    for t in range(HEADS // per):
        tile = slice(t * LANES, (t + 1) * LANES)
        total = None
        for e in range(per):
            h = t * per + e
            mask = (lane == e).astype(F32).astype(BF16)
            scores = nt(q_ref[rows, tile] * mask, k_ref[:, tile])
            if bias_of is not None:
                scores = scores + bias_of(h)
            top = jnp.max(scores, axis=-1, keepdims=True)
            raised = jnp.exp(scores - top)
            scale = 1.0 / jnp.sum(raised, axis=-1, keepdims=True)
            weights = (raised * scale).astype(BF16)
            part = nn(weights, v_ref[:, tile] * mask)
            total = part if total is None else total + part
        out.append(total)
    return out


def row_kernel(msa_ref, bias_ref, drop_ref, w_ref, wo_ref, out_ref, wide, bias, q, k, v, g, res, stage):
    seqs, length, width = msa_ref.shape
    pairs = length // 2
    for t in range(2):
        wide[t] = bias_ref[t].astype(F32).reshape(length * HEADS, LANES)
    for h in range(HEADS):
        for t in range(2):
            tile = slice(t * LANES, (t + 1) * LANES)
            bias[h, :, tile] = wide[t, pl.ds(h, length, stride=HEADS), :]

    def one(s, carry):
        token = msa_ref[s].astype(F32)
        m1 = norm(token).astype(BF16)
        q[...] = (nn(m1, w_ref[:, 0:width]) * WIDTH ** (-0.5)).astype(BF16)
        k[...] = nn(m1, w_ref[:, width : 2 * width]).astype(BF16)
        v[...] = nn(m1, w_ref[:, 2 * width : 3 * width]).astype(BF16)
        g[...] = nn(m1, w_ref[:, 3 * width : 4 * width])
        heads = jnp.concatenate(heads_of(q, k, v, slice(None), lambda h: bias[h]), axis=-1)
        gated = (jax.nn.sigmoid(g[...]) * heads).astype(BF16)
        change = nn(gated, wo_ref[...])
        after = token + drop_ref[...].astype(F32) * (1.0 / 0.9) * change
        for t in range(2):
            res[t] = after[:, t * LANES : (t + 1) * LANES]
            for r in range(2):
                stage[t, pl.ds(s * 2 + r, pairs, stride=seqs * 2), :] = res[t, pl.ds(r, pairs, stride=2), :]
        return carry

    lax.fori_loop(0, seqs, one, 0)
    for t in range(2):
        out_ref[t] = stage[t].reshape(out_ref.shape[1:]).astype(BF16)


def exchange_kernel(src, dst, mid0, mid1, keep_sem, s0, r0, s1, r1, s2, r2, s3, r3):
    x, y, c = here()
    yc = y * NC + c
    a = keep(src.at[0, x], mid0.at[x], keep_sem.at[0])
    b = keep(src.at[1, :, yc], mid1.at[yc], keep_sem.at[1])
    wy = wide_y(x, y, c)
    greet([p for _, p, _, _ in wy] + x_peers(x, y, c))
    first0 = [
        push(src.at[0, (x + k) % NX], mid0.at[x], s0.at[k - 1], r0.at[k - 1], place((x + k) % NX, y, c))
        for k in RING_ORDER
    ]
    first1 = [
        push(src.at[1, :, yy * NC + cc], mid1.at[yc], s1.at[n], r1.at[n], p) for n, p, yy, cc in wy
    ]
    a.wait()
    b.wait()
    for m in first0:
        m.wait_recv()
    second0 = [
        push(mid0.at[:, yy * NC + cc], dst.at[0, :, yc], s2.at[n], r2.at[n], p) for n, p, yy, cc in wy
    ]
    a = keep(mid0.at[:, yc], dst.at[0, :, yc], keep_sem.at[0])
    for m in first1:
        m.wait_recv()
    second1 = [
        push(mid1.at[:, (x + k) % NX], dst.at[1, x], s3.at[k - 1], r3.at[k - 1], place((x + k) % NX, y, c))
        for k in RING_ORDER
    ]
    b = keep(mid1.at[:, x], dst.at[1, x], keep_sem.at[1])
    a.wait()
    b.wait()
    for m in second0 + second1:
        m.wait_recv()
    for m in first0 + first1 + second0 + second1:
        m.wait_send()


def column_kernel(in_ref, w_ref, wo_ref, flank_ref, out_ref, left_ref, right_ref, both, q, k, v, g, acc):
    width = w_ref.shape[0]
    tokens = out_ref.shape[0]
    seqs = tokens // 2
    for t in range(2):
        both[t] = in_ref[t].astype(F32).reshape(tokens, LANES)

    def one(r, carry):
        token = jnp.concatenate([both[t, pl.ds(r, seqs, stride=2), :] for t in range(2)], axis=-1)
        m3 = norm(token).astype(BF16)
        q[...] = (nn(m3, w_ref[:, 0:width]) * WIDTH ** (-0.5)).astype(BF16)
        k[...] = nn(m3, w_ref[:, width : 2 * width]).astype(BF16)
        v[...] = nn(m3, w_ref[:, 2 * width : 3 * width]).astype(BF16)
        g[...] = nn(m3, w_ref[:, 3 * width : 4 * width])
        step = 256

        def chunk(n, inner):
            rows = pl.ds(pl.multiple_of(n * step, step), step)
            heads = jnp.concatenate(heads_of(q, k, v, rows, None), axis=-1)
            acc[rows, :] = (jax.nn.sigmoid(g[rows, :]) * heads).astype(BF16)
            return inner

        lax.fori_loop(0, seqs // step, chunk, 0)
        after = (token + nn(acc[...], wo_ref[...])).astype(BF16).astype(F32)
        for t in range(2):
            both[t, pl.ds(r, seqs, stride=2), :] = after[:, t * LANES : (t + 1) * LANES]
        m4 = norm(after).astype(BF16)
        factors = nt(flank_ref[...], m4).astype(BF16)
        left_ref[r] = factors[:FACTORS]
        right_ref[r] = factors[FACTORS:]
        return carry

    lax.fori_loop(0, 2, one, 0)
    for t in range(2):
        out_ref[:, t * LANES : (t + 1) * LANES] = both[t].astype(BF16)


def outer_kernel(
    left, right, exit_ref, change, lefts, rights, others, prod, wide, diag, tile, arrive, land,
    keep_sem, s0, r0, s1, r1, s2, r2, s3, r3,
):
    x, y, c = here()
    own = [keep(left, lefts.at[y], keep_sem.at[0]), keep(right, rights.at[x], keep_sem.at[1])]
    other = place(x, y, 1 - c)
    greet(y_peers(x, y, c) + x_peers(x, y, c) + [other])
    fl = [
        push(left, lefts.at[y], s0.at[k - 1], r0.at[k - 1], place(x, (y + k) % NY, c)) for k in RING_ORDER
    ]
    fr = [
        push(right, rights.at[x], s1.at[k - 1], r1.at[k - 1], place((x + k) % NX, y, c)) for k in RING_ORDER
    ]
    swap = [push(right, others.at[x], s2.at[NX - 1], r2.at[NX - 1], other)]

    depth = exit_ref.shape[1]
    per = LANES // FACTORS
    wide[...] = exit_ref[...].astype(F32)
    diag[...] = jnp.zeros_like(diag)
    for d in range(FACTORS):
        block = wide[pl.ds(d, FACTORS, stride=FACTORS), :].astype(BF16)
        for e in range(per):
            diag[d, e * FACTORS : (e + 1) * FACTORS, e * depth : (e + 1) * depth] = block

    for n in reversed(range(NX - 1)):
        k = RING_ORDER[n]
        fr[n].wait_recv()
        xs = (x + NX - k) % NX
        swap.append(push(rights.at[xs], others.at[xs], s2.at[k - 1], r2.at[k - 1], other))
    for m in own:
        m.wait()
    for m in fl:
        m.wait_recv()

    seqs = left.shape[1]
    rows = rights.shape[0] * rights.shape[1]
    js = rows // FACTORS
    pitch = FACTORS + 8
    cols = lefts[...].reshape(lefts.shape[0] * lefts.shape[1], seqs)
    lots = cols.shape[0] // LANES

    def fill(source, base):
        both = source[...].reshape(rows, seqs)
        out = nt(both, cols) * (1.0 / seqs)
        for n in range(js):
            for u in range(lots):
                at = pl.ds(pl.multiple_of((base + n) * pitch, 8), FACTORS)
                prod[u, at, :] = out[n * FACTORS : (n + 1) * FACTORS, u * LANES : (u + 1) * LANES]

    fill(rights, c * js)
    for m in swap:
        m.wait_recv()
    fill(others, (1 - c) * js)
    for e in range(per):
        tile[e] = jnp.zeros(tile.shape[1:], F32)

    def step(d, carry):
        lhs = jnp.concatenate(
            [prod[u, pl.ds(d, 2 * js, stride=pitch), :] for u in range(lots)], axis=0
        ).astype(BF16)
        add = nn(lhs, diag[d])
        for e in range(per):
            tile[e, : lots * 2 * js, :] += add[:, e * depth : (e + 1) * depth]
        return carry

    lax.fori_loop(0, FACTORS, step, 0)
    for u in range(lots):
        for e in range(per):
            i = u * per + e
            arrive[i // 2, i % 2] = tile[e, u * 2 * js : (u + 1) * 2 * js, :].astype(BF16)
    own = keep(arrive.at[y], land.at[y], keep_sem.at[0])
    back = [
        push(arrive.at[(y + k) % NY], land.at[y], s3.at[k - 1], r3.at[k - 1], place(x, (y + k) % NY, c))
        for k in RING_ORDER
    ]
    own.wait()
    for m in back:
        m.wait_recv()
    for t in range(2):
        for yy in range(NY):
            tile[t, yy * 2 * js : (yy + 1) * 2 * js, :] = land[yy, t].astype(F32)
            for cc in range(NC):
                for r in range(2):
                    change[t, pl.ds((yy * NC + cc) * 2 + r, NX, stride=NY * NC * 2), :] = tile[
                        t, pl.ds(yy * 2 * js + cc * js + r, NX, stride=2), :
                    ]
    for m in fl + fr + swap + back:
        m.wait_send()


def sems(*counts):
    out = []
    for n in counts:
        out += [pltpu.SemaphoreType.DMA((n,)), pltpu.SemaphoreType.DMA((n,))]
    return out


def remote(number):
    return pltpu.CompilerParams(collective_id=number, has_side_effects=True, vmem_limit_bytes=LIMIT)


def shards(msa, pair, drop, w_bias, w_row, wo_row, w_col, wo_col, flanks, w_exit):
    seqs, length, width = msa.shape
    rows, _, depth = pair.shape
    everyone = NX * NY * NC
    wide = NY * NC - 1
    local = pltpu.CompilerParams(vmem_limit_bytes=LIMIT)
    own = pl.pallas_call(
        bias_rows_kernel,
        out_shape=jax.ShapeDtypeStruct((2, rows * HEADS, LANES), BF16),
        in_specs=[VMEM] * 2,
        out_specs=VMEM,
        compiler_params=local,
    )(pair.reshape(rows * length, depth), w_bias.T)
    bias = pl.pallas_call(
        bias_gather_kernel,
        out_shape=jax.ShapeDtypeStruct((2, NX, NY * NC, rows * HEADS, LANES), BF16),
        in_specs=[VMEM],
        out_specs=VMEM,
        scratch_shapes=[pltpu.SemaphoreType.DMA((2,))]
        + sems(wide, wide, NX - 1, NY - 1, NX - 1, NY - 1),
        compiler_params=remote(0),
    )(own)
    msa2 = pl.pallas_call(
        row_kernel,
        out_shape=jax.ShapeDtypeStruct((2, NX, NY * NC, seqs * rows, LANES), BF16),
        in_specs=[VMEM] * 5,
        out_specs=VMEM,
        scratch_shapes=[
            pltpu.VMEM((2, length * HEADS, LANES), F32),
            pltpu.VMEM((HEADS, length, length), F32),
            pltpu.VMEM((length, width), BF16),
            pltpu.VMEM((length, width), BF16),
            pltpu.VMEM((length, width), BF16),
            pltpu.VMEM((length, width), F32),
            pltpu.VMEM((2, length, LANES), F32),
            pltpu.VMEM((2, seqs * length, LANES), F32),
        ],
        compiler_params=local,
    )(msa, bias, drop, w_row, wo_row)
    turned = pl.pallas_call(
        exchange_kernel,
        out_shape=jax.ShapeDtypeStruct(msa2.shape, BF16),
        in_specs=[VMEM],
        out_specs=VMEM,
        scratch_shapes=[
            pltpu.VMEM((NX, NY * NC, seqs * rows, LANES), BF16),
            pltpu.VMEM((NY * NC, NX, seqs * rows, LANES), BF16),
            pltpu.SemaphoreType.DMA((2,)),
        ]
        + sems(NX - 1, wide, wide, NX - 1),
        compiler_params=remote(1),
    )(msa2)
    total = seqs * everyone
    aligned, left, right = pl.pallas_call(
        column_kernel,
        out_shape=(
            jax.ShapeDtypeStruct((total * rows, width), BF16),
            jax.ShapeDtypeStruct((rows, FACTORS, total), BF16),
            jax.ShapeDtypeStruct((rows, FACTORS, total), BF16),
        ),
        in_specs=[VMEM] * 4,
        out_specs=(VMEM,) * 3,
        scratch_shapes=[
            pltpu.VMEM((2, total * rows, LANES), F32),
            pltpu.VMEM((total, width), BF16),
            pltpu.VMEM((total, width), BF16),
            pltpu.VMEM((total, width), BF16),
            pltpu.VMEM((total, width), F32),
            pltpu.VMEM((total, width), BF16),
        ],
        compiler_params=local,
    )(turned, w_col, wo_col, flanks.T)
    chunk = (rows * FACTORS, total)
    js = NX * rows
    lots = NY * rows * FACTORS // LANES
    change = pl.pallas_call(
        outer_kernel,
        out_shape=jax.ShapeDtypeStruct(pair.shape, F32),
        in_specs=[VMEM] * 3,
        out_specs=VMEM,
        scratch_shapes=[
            pltpu.VMEM((NY,) + chunk, BF16),
            pltpu.VMEM((NX,) + chunk, BF16),
            pltpu.VMEM((NX,) + chunk, BF16),
            pltpu.VMEM((lots, 2 * js * (FACTORS + 8), LANES), F32),
            pltpu.VMEM(w_exit.shape, F32),
            pltpu.VMEM((FACTORS, LANES, (LANES // FACTORS) * depth), BF16),
            pltpu.VMEM((LANES // FACTORS, max(lots, NY) * 2 * js, depth), F32),
            pltpu.VMEM((NY, rows, 2 * js, depth), BF16),
            pltpu.VMEM((NY, rows, 2 * js, depth), BF16),
            pltpu.SemaphoreType.DMA((2,)),
        ]
        + sems(NY - 1, NX - 1, NX, NY - 1),
        compiler_params=remote(2),
    )(left.reshape(chunk), right.reshape(chunk), w_exit)
    return aligned.reshape(total, rows, width), (pair.astype(F32) + change).astype(BF16)


def solution(mesh):
    torus = Mesh(mesh.devices.reshape(mesh.shape["groups"], NX, NY, NC), GROUPS_DAP)
    return jax.shard_map(
        shards,
        mesh=torus,
        in_specs=(
            P(GROUPS_DAP, None, None),
            P(GROUPS_DAP, None, None),
            P("groups", None),
        )
        + (P(),) * 7,
        out_specs=(P("groups", DAP, None), P(GROUPS_DAP, None, None)),
        check_vma=False,
    )
```

time: 368 us -> 132 us (0.36)
  waiting for transfers between devices: 124 us -> 0 us
  Pallas kernels: 30.7 us -> 127 us
  local copies, waits for them, and re-layouts: 60.6 us -> 2.03 us
  matrix products: 52.1 us -> 0 us
  blocking collectives: 51.8 us -> 0 us
  other arithmetic: 16.8 us -> 1.63 us
  starting transfers between devices: 14.8 us -> 0 us
  between operations: 14.4 us -> 0.66 us
    pallas_call x0 -> x6, Pallas kernels: none -> 127 us  [the longest x1 39.7 us: shards(): pl.pallas_call(bias_gather_kernel, out_shape=jax.ShapeDtypeStruct((2, NX,...]
    all_gather x2 -> x0, waiting for transfers between devices: 105 us -> none  [the longest x1 77.3 us: shards(): piece = lax.all_gather(right, DAP, axis=1, tiled=True)]
    all_gather x2 -> x0, blocking collectives: 51.8 us -> none  [stacked_from(): tiles = lax.all_gather(tiles, axes[k], axis=0, tiled=True)]
    dot_general x24 -> x0, matrix products: 41.1 us -> none  [the longest x8 14.8 us: one_head(): jnp.einsum('bij,bjd->bid', weights, vh, preferred_element_type=jnp.float32)]
    dot_general x8 -> x0, Pallas kernels: 30.7 us -> none  [one_head(): jnp.einsum('bij,bjd->bid', weights, vh, preferred_element_type=jnp.float32)]
    dynamic_slice x40 -> x0, local copies, waits for them, and re-layouts: 27.3 us -> none  [attend(): lax.map(one_head, (jnp.moveaxis(query, 2, 0), jnp.moveaxis(keys, 2, 0), j...]
    all_to_all x1 -> x0, waiting for transfers between devices: 18.9 us -> none  [shards(): lax.all_to_all(homolog_later, DAP, split_axis=1, concat_axis=0, tiled=True)]
    dynamic_update_slice x16 -> x0, local copies, waits for them, and re-layouts: 15 us -> none  [attend(): lax.map(one_head, (jnp.moveaxis(query, 2, 0), jnp.moveaxis(keys, 2, 0), j...]
  transfers between devices with their start and end apart: 3 -> 0, of which waited for: 3 -> 0; matrix products, arithmetic and copies ran while one was open for 2% -> 0% of each run, Pallas kernels for 0% -> 0%
where the time goes in v1:
time: 132 us; the launch traced here: 131 us
  Pallas kernels  127 us (96%)
  local copies, waits for them, and re-layouts  2.03 us (2%)
  other arithmetic  1.63 us (1%)
    pallas_call x1, Pallas kernels, shards(): pl.pallas_call(bias_gather_kernel, out_shape=jax.ShapeDtypeStruct((2, NX,...  39.7 us
    pallas_call x1, Pallas kernels, shards(): pl.pallas_call(outer_kernel, out_shape=jax.ShapeDtypeStruct(pair.shape, F...  33.5 us
    pallas_call x1, Pallas kernels, shards(): pl.pallas_call(exchange_kernel, out_shape=jax.ShapeDtypeStruct(msa2.shape...  21.1 us
    pallas_call x1, Pallas kernels, shards(): pl.pallas_call(column_kernel, out_shape=(jax.ShapeDtypeStruct((total * ro...  17.5 us
    pallas_call x1, Pallas kernels, shards(): pl.pallas_call(row_kernel, out_shape=jax.ShapeDtypeStruct((2, NX, NY * NC...  13.3 us

profile of v1, /device:TPU:513, one launch (start us, length us, event | category | flops | bytes accessed | tf_op | source)
XLA Modules:
  0.0 131.3 jit_solution(12714072025557549479)
XLA Ops:
  0.6 1.9 %shard_map.113.own = bf16[2,16,128]{2,1,0:T(8,128)(2,1)} custom-call(bf16[512,128]{1,0:T(8,128)(2,1)} %bitcast.5, bf16[8,128]{1,0:T(8,128)(2,1)} %bitcast.9), custom_call_target="tpu_custom_call" | custom-call | tf_op jit(solution)/shard_map/pallas_call | solution.py:383
  2.5 39.7 %shard_map.114.bias_ref = bf16[2,8,16,16,128]{4,3,2,1,0:T(8,128)(2,1)} custom-call(bf16[2,16,128]{2,1,0:T(8,128)(2,1)} %shard_map.113.own), custom_call_target="tpu_custom_call" | custom-call | tf_op jit(solution)/shard_map/pallas_call | solution.py:390
  42.2 13.3 %shard_map.115.src = bf16[2,8,16,8,128]{4,3,2,1,0:T(8,128)(2,1)} custom-call(bf16[4,256,256]{2,1,0:T(8,128)(2,1)} %msa_ref.1, bf16[2,8,16,16,128]{4,3,2,1,0:T(8,128)(2,1)} %shard_map.114.bias_ref, s32[256,256]{1,0:T(8,128)} %drop_ref.1, bf16[256,1024]{1,0:T(8,128)(2,1)} %w_ref.2, bf16[256,256]{1,0:T(8,128)(2,1)} %wo_ref.2), custom_call_target="tpu_custom_call" | custom-call | tf_op jit(solution)/shard_map/pallas_call | solution.py:399
  55.5 21.1 %shard_map.116.in_ref = bf16[2,8,16,8,128]{4,3,2,1,0:T(8,128)(2,1)} custom-call(bf16[2,8,16,8,128]{4,3,2,1,0:T(8,128)(2,1)} %shard_map.115.src), custom_call_target="tpu_custom_call" | custom-call | tf_op jit(solution)/shard_map/pallas_call | solution.py:416
  76.7 17.5 %shard_map.117 = (bf16[1024,256]{1,0:T(8,128)(2,1)}, bf16[2,32,512]{2,1,0:T(8,128)(2,1)}, bf16[2,32,512]{2,1,0:T(8,128)(2,1)}) custom-call(bf16[2,8,16,8,128]{4,3,2,1,0:T(8,128)(2,1)} %shard_map.116.in_ref, bf16[256,1024]{1,0:T(8,128)(2,1)} %w_ref.3, bf16[256,256]{1,0:T(8,128)(2,1)} %wo_ref.3, bf16[64,256]{1,0:T(8,128)(2,1)} %bitcast.8), custom_call_target="tpu_custom_call" | custom-call | tf_op jit(solution)/shard_map/pallas_call | solution.py:430
  94.2 2.0 %reshape.17 = bf16[512,2,256]{2,1,0:T(2,128)(2,1)} reshape(bf16[1024,256]{1,0:T(8,128)(2,1)} %get-tuple-element.5) | data formatting | bytes 1048576 | tf_op jit(solution)/shard_map/reshape | solution.py:472
  96.2 0.0 copy-start
  96.2 33.5 %shard_map.118 = f32[2,256,128]{2,1,0:T(8,128)} custom-call(bf16[64,512]{1,0:T(8,128)(2,1)} %bitcast.6, bf16[64,512]{1,0:T(8,128)(2,1)} %bitcast.7, bf16[1024,128]{1,0:T(8,128)(2,1)} %exit_ref.1), custom_call_target="tpu_custom_call" | custom-call | tf_op jit(solution)/shard_map/pallas_call | solution.py:452
  129.7 0.0 copy-done
  129.7 1.6 %add_convert_fusion = bf16[2,256,128]{2,1,0:T(8,128)(2,1)} fusion(f32[2,256,128]{2,1,0:T(8,128)} %shard_map.118, bf16[2,256,128]{2,1,0:T(8,128)(2,1)S(1)} %copy-done), kind=kLoop, calls=%fused_computation | loop fusion | flops 196608 | bytes 524288 | tf_op jit(solution)/shard_map/convert_element_type | solution.py:472
Async XLA Ops:
  96.2 33.5 %copy-start = (bf16[2,256,128]{2,1,0:T(8,128)(2,1)S(1)}, bf16[2,256,128]{2,1,0:T(8,128)(2,1)}, u32[]{:S(2)}) copy-start(bf16[2,256,128]{2,1,0:T(8,128)(2,1)} %param.11) | copy-start | bytes 393220

commit v2 on v1

v2 whole, which is shorter than its diff:
```python
import jax
import jax.numpy as jnp
from jax import lax
from jax.experimental import pallas as pl
from jax.experimental.pallas import tpu as pltpu
from jax.sharding import Mesh
from jax.sharding import PartitionSpec as P

HEADS = 8
WIDTH = 32
FACTORS = 32
NX, NY, NC = 8, 8, 2
LANES = 128
GROUPS_DAP = ("groups", "dap_0", "dap_1", "dap_2")
DAP = ("dap_0", "dap_1", "dap_2")
MESH = pl.DeviceIdType.MESH
F32, BF16 = jnp.float32, jnp.bfloat16
VMEM = pl.BlockSpec(memory_space=pltpu.VMEM)
LIMIT = 60 * 1024 * 1024
RING_ORDER = (4, 3, 5, 2, 6, 1, 7)


def norm(v):
    center = v - jnp.mean(v, axis=-1, keepdims=True)
    spread = jnp.mean(center * center, axis=-1, keepdims=True)
    return center * lax.rsqrt(spread + 1e-05)


def nt(a, b):
    return lax.dot_general(a, b, (((1,), (1,)), ((), ())), preferred_element_type=F32)


def nn(a, b):
    return jnp.dot(a, b, preferred_element_type=F32)


def here():
    return lax.axis_index("dap_0"), lax.axis_index("dap_1"), lax.axis_index("dap_2")


def place(x, y, c):
    return {"dap_0": x, "dap_1": y, "dap_2": c}


def knock(peers):
    sem = pltpu.get_barrier_semaphore()
    for peer in peers:
        pl.semaphore_signal(sem, inc=1, device_id=peer, device_id_type=MESH)
    return len(peers)


def answered(count):
    pl.semaphore_wait(pltpu.get_barrier_semaphore(), count)


def x_peers(x, y, c):
    return [place((x + k) % NX, y, c) for k in RING_ORDER]


def y_peers(x, y, c):
    return [place(x, (y + k) % NY, c) for k in RING_ORDER]


def push(src, dst, send, recv, peer):
    copy = pltpu.make_async_remote_copy(
        src_ref=src, dst_ref=dst, send_sem=send, recv_sem=recv, device_id=peer, device_id_type=MESH
    )
    copy.start()
    return copy


def keep(src, dst, sem):
    copy = pltpu.make_async_copy(src, dst, sem)
    copy.start()
    return copy


def wide_y(x, y, c):
    out = [(NY * NC - 2, place(x, y, 1 - c), y, 1 - c)]
    for k in RING_ORDER:
        for f in range(NC):
            cc = (c + f) % NC
            yy = (y + k) % NY
            out.append((2 * (k - 1) + f, place(x, yy, cc), yy, cc))
    return out


def wide_x(x, y, c):
    out = [(NX * NC - 2, place(x, y, 1 - c), x, 1 - c)]
    for k in RING_ORDER:
        for f in range(NC):
            cc = (c + f) % NC
            xx = (x + k) % NX
            out.append((2 * (k - 1) + f, place(xx, y, cc), xx, cc))
    return out


def softmax_product(scores, v):
    raised = jnp.exp(scores - jnp.max(scores, axis=-1, keepdims=True)).astype(BF16)
    both = nn(raised, jnp.concatenate([v, jnp.ones_like(v)], axis=-1))
    return both[:, :LANES] / both[:, LANES:]


def head(h):
    per = LANES // WIDTH
    lane = lax.broadcasted_iota(jnp.int32, (1, LANES), 1) // WIDTH
    mask = (lane == h % per).astype(F32).astype(BF16)
    return slice(h // per * LANES, (h // per + 1) * LANES), mask


def merge(parts):
    per = LANES // WIDTH
    tiles = []
    for t in range(HEADS // per):
        total = parts[t * per]
        for e in range(1, per):
            total = total + parts[t * per + e]
        tiles.append(total)
    return jnp.concatenate(tiles, axis=-1)


def row_kernel(
    pair_ref, wb_ref, msa_ref, drop_ref, w_ref, wo_ref, dst,
    own, full, wide, bias, q, k, v, g, raw, res, stage, src, mid0, mid1, keep_sem,
    s0, r0, s1, r1, s2, r2, s3, r3, s4, r4, s5, r5, e0, f0, e1, f1, e2, f2, e3, f3,
):
    seqs, length, width = msa_ref.shape
    pairs = length // 2
    x, y, c = here()
    yc = y * NC + c
    wy, wx = wide_y(x, y, c), wide_x(x, y, c)
    count = knock([p for _, p, _, _ in wy] + [p for _, p, _, _ in wx[1:]])

    zn = norm(pair_ref[...].astype(F32)).astype(BF16)
    rows = nt(wb_ref[...], zn)
    rows = jnp.concatenate([rows[:, :length], rows[:, length:]], axis=0).astype(BF16)
    for t in range(2):
        own[t] = rows[:, t * LANES : (t + 1) * LANES]
    answered(count)

    mine = [keep(own.at[t], full.at[t, x, yc], keep_sem.at[t]) for t in range(2)]
    first0 = [push(own.at[0], full.at[0, x, yc], s0.at[n], r0.at[n], p) for n, p, _, _ in wy]
    first1 = [push(own.at[1], full.at[1, x, yc], s1.at[n], r1.at[n], p) for n, p, _, _ in wx]

    def project(s, carry):
        m1 = norm(msa_ref[s].astype(F32)).astype(BF16)
        q[s] = (nn(m1, w_ref[:, 0:width]) * WIDTH ** (-0.5)).astype(BF16)
        k[s] = nn(m1, w_ref[:, width : 2 * width]).astype(BF16)
        v[s] = nn(m1, w_ref[:, 2 * width : 3 * width]).astype(BF16)
        g[s] = nn(m1, w_ref[:, 3 * width : 4 * width])
        return carry

    lax.fori_loop(0, seqs, project, 0)
    for m in mine:
        m.wait()
    for m in first0:
        m.wait_recv()
    half = pl.ds(c * NY, NY)
    second0 = [
        push(full.at[0, x, half], full.at[0, x, half], s2.at[n - 1], r2.at[n - 1], place((x + n) % NX, y, c))
        for n in RING_ORDER
    ]
    for m in first1:
        m.wait_recv()
    halfx, pair = pl.ds(c * (NX // 2), NX // 2), pl.ds(y * NC, NC)
    second1 = [
        push(full.at[1, halfx, pair], full.at[1, halfx, pair], s3.at[n - 1], r3.at[n - 1], place(x, (y + n) % NY, c))
        for n in RING_ORDER
    ]

    def score(s, carry):
        for h in range(HEADS):
            tile, mask = head(h)
            raw[s, h] = nt(q[s, :, tile] * mask, k[s, :, tile])
        return carry

    lax.fori_loop(0, seqs, score, 0)
    other = place(x, y, 1 - c)
    third = []
    for n in reversed(range(NX - 1)):
        d = RING_ORDER[n]
        second0[n].wait_recv()
        xs = (x + NX - d) % NX
        third.append(push(full.at[0, xs, half], full.at[0, xs, half], s4.at[d - 1], r4.at[d - 1], other))
        second1[n].wait_recv()
        pairs_of = pl.ds(((y + NY - d) % NY) * NC, NC)
        third.append(
            push(full.at[1, halfx, pairs_of], full.at[1, halfx, pairs_of], s5.at[d - 1], r5.at[d - 1], other)
        )
    for m in third:
        m.wait_recv()
    for t in range(2):
        wide[t] = full[t].astype(F32).reshape(length * HEADS, LANES)
    for h in range(HEADS):
        for t in range(2):
            bias[h, :, t * LANES : (t + 1) * LANES] = wide[t, pl.ds(h, length, stride=HEADS), :]

    chunks = src.shape[0]
    group = seqs // chunks
    sent = first0 + first1 + second0 + second1 + third
    hops = []
    for n in range(chunks):

        def one(i, carry):
            s = n * group + i
            parts = []
            for h in range(HEADS):
                tile, mask = head(h)
                parts.append(softmax_product(raw[s, h] + bias[h], v[s, :, tile] * mask))
            gated = (jax.nn.sigmoid(g[s]) * merge(parts)).astype(BF16)
            change = nn(gated, wo_ref[...])
            after = msa_ref[s].astype(F32) + drop_ref[...].astype(F32) * (1.0 / 0.9) * change
            for t in range(2):
                res[t] = after[:, t * LANES : (t + 1) * LANES]
                for r in range(2):
                    stage[t, pl.ds(i * 2 + r, pairs, stride=8), :] = res[t, pl.ds(r, pairs, stride=2), :]
            return carry

        lax.fori_loop(0, group, one, 0)
        for t in range(2):
            value = stage[t].reshape(NX, NY * NC, 8, LANES)[:, :, : group * 2, :]
            src[n, t] = value.astype(BF16)
        h0 = [
            push(src.at[n, 0, (x + d) % NX], mid0.at[n, x], e0.at[n, d - 1], f0.at[n, d - 1], place((x + d) % NX, y, c))
            for d in RING_ORDER
        ]
        h1 = [
            push(src.at[n, 1, :, yy * NC + cc], mid1.at[n, yc], e1.at[n, m], f1.at[n, m], p) for m, p, yy, cc in wy
        ]
        a = keep(src.at[n, 0, x], mid0.at[n, x], keep_sem.at[2 * n])
        b = keep(src.at[n, 1, :, yc], mid1.at[n, yc], keep_sem.at[2 * n + 1])
        hops.append((h0, h1, a, b))
    last = []
    for n, (h0, h1, a, b) in enumerate(hops):
        a.wait()
        b.wait()
        for m in h0:
            m.wait_recv()
        g0 = [
            push(mid0.at[n, :, yy * NC + cc], dst.at[0, :, yc, n], e2.at[n, m], f2.at[n, m], p)
            for m, p, yy, cc in wy
        ]
        a = keep(mid0.at[n, :, yc], dst.at[0, :, yc, n], keep_sem.at[2 * n])
        for m in h1:
            m.wait_recv()
        g1 = [
            push(mid1.at[n, :, (x + d) % NX], dst.at[1, x, :, n], e3.at[n, d - 1], f3.at[n, d - 1], place((x + d) % NX, y, c))
            for d in RING_ORDER
        ]
        b = keep(mid1.at[n, :, x], dst.at[1, x, :, n], keep_sem.at[2 * n + 1])
        last.append((g0, g1, a, b))
        sent += h0 + h1 + g0 + g1
    for g0, g1, a, b in last:
        a.wait()
        b.wait()
        for m in g0 + g1:
            m.wait_recv()
    for m in sent:
        m.wait_send()


def column_kernel(
    in_ref, w_ref, wo_ref, flank_ref, exit_ref, out_ref, change,
    both, q, k, v, g, left, right, lefts, rights, others, prod, wide, diag, tile, arrive, land,
    keep_sem, s0, r0, s1, r1, s2, r2, s3, r3,
):
    width = w_ref.shape[0]
    tokens = out_ref.shape[0]
    seqs = tokens // 2
    x, y, c = here()
    other = place(x, y, 1 - c)
    count = knock(y_peers(x, y, c) + x_peers(x, y, c) + [other])
    for t in range(2):
        both[t] = in_ref[t].astype(F32).reshape(tokens, LANES)
    sent, moves = [], []
    for r in range(2):
        token = jnp.concatenate([both[t, pl.ds(r, seqs, stride=2), :] for t in range(2)], axis=-1)
        m3 = norm(token).astype(BF16)
        q[...] = (nn(m3, w_ref[:, 0:width]) * WIDTH ** (-0.5)).astype(BF16)
        k[...] = nn(m3, w_ref[:, width : 2 * width]).astype(BF16)
        v[...] = nn(m3, w_ref[:, 2 * width : 3 * width]).astype(BF16)
        g[...] = nn(m3, w_ref[:, 3 * width : 4 * width])
        parts = []
        for h in range(HEADS):
            part, mask = head(h)
            parts.append(softmax_product(nt(q[:, part] * mask, k[:, part]), v[:, part] * mask))
        gated = (jax.nn.sigmoid(g[...]) * merge(parts)).astype(BF16)
        after = (token + nn(gated, wo_ref[...])).astype(BF16).astype(F32)
        for t in range(2):
            both[t, pl.ds(r, seqs, stride=2), :] = after[:, t * LANES : (t + 1) * LANES]
        factors = nt(flank_ref[...], norm(after).astype(BF16)).astype(BF16)
        left[r] = factors[:FACTORS]
        right[r] = factors[FACTORS:]
        if r == 0:
            answered(count)
        own = [keep(left.at[r], lefts.at[y, r], keep_sem.at[2 * r]), keep(right.at[r], rights.at[x, r], keep_sem.at[2 * r + 1])]
        fl = [
            push(left.at[r], lefts.at[y, r], s0.at[r, d - 1], r0.at[r, d - 1], place(x, (y + d) % NY, c))
            for d in RING_ORDER
        ]
        fr = [
            push(right.at[r], rights.at[x, r], s1.at[r, d - 1], r1.at[r, d - 1], place((x + d) % NX, y, c))
            for d in RING_ORDER
        ]
        swap = [push(right.at[r], others.at[x, r], s2.at[r, NX - 1], r2.at[r, NX - 1], other)]
        moves.append((own, fl, fr, swap))

    for t in range(2):
        out_ref[:, t * LANES : (t + 1) * LANES] = both[t].astype(BF16)
    depth = exit_ref.shape[1]
    per = LANES // FACTORS
    wide[...] = exit_ref[...].astype(F32)
    diag[...] = jnp.zeros_like(diag)
    for d in range(FACTORS):
        block = wide[pl.ds(d, FACTORS, stride=FACTORS), :].astype(BF16)
        for e in range(per):
            diag[d, e * FACTORS : (e + 1) * FACTORS, e * depth : (e + 1) * depth] = block

    for r, (own, fl, fr, swap) in enumerate(moves):
        for n in reversed(range(NX - 1)):
            d = RING_ORDER[n]
            fr[n].wait_recv()
            xs = (x + NX - d) % NX
            swap.append(push(rights.at[xs, r], others.at[xs, r], s2.at[r, d - 1], r2.at[r, d - 1], other))
        for m in own:
            m.wait()
        for m in fl:
            m.wait_recv()
        sent += fl + fr + swap

    rows = rights.shape[0] * rights.shape[1] * rights.shape[2]
    js = rows // FACTORS
    pitch = FACTORS + 8
    cols = lefts[...].reshape(rows, seqs)
    lots = rows // LANES

    def fill(source, base):
        out = nt(source[...].reshape(rows, seqs), cols) * (1.0 / seqs)
        for n in range(js):
            for u in range(lots):
                at = pl.ds(pl.multiple_of((base + n) * pitch, 8), FACTORS)
                prod[u, at, :] = out[n * FACTORS : (n + 1) * FACTORS, u * LANES : (u + 1) * LANES]

    fill(rights, c * js)
    for _, _, _, swap in moves:
        for m in swap:
            m.wait_recv()
    fill(others, (1 - c) * js)
    for d in range(FACTORS):
        tile[:, d * LANES : (d + 1) * LANES] = jnp.concatenate(
            [prod[u, pl.ds(d, 2 * js, stride=pitch), :] for u in range(lots)], axis=0
        ).astype(BF16)
    update = nn(tile[...], diag[...].reshape(FACTORS * LANES, per * depth))
    for u in range(lots):
        for e in range(per):
            i = u * per + e
            arrive[i // 2, i % 2] = update[u * 2 * js : (u + 1) * 2 * js, e * depth : (e + 1) * depth].astype(BF16)
    own = keep(arrive.at[y], land.at[y], keep_sem.at[0])
    back = [
        push(arrive.at[(y + d) % NY], land.at[y], s3.at[d - 1], r3.at[d - 1], place(x, (y + d) % NY, c))
        for d in RING_ORDER
    ]
    own.wait()
    for m in back:
        m.wait_recv()
    for t in range(2):
        for yy in range(NY):
            prod[t, yy * 2 * js : (yy + 1) * 2 * js, :] = land[yy, t].astype(F32)
            for cc in range(NC):
                for r in range(2):
                    change[t, pl.ds((yy * NC + cc) * 2 + r, NX, stride=NY * NC * 2), :] = prod[
                        t, pl.ds(yy * 2 * js + cc * js + r, NX, stride=2), :
                    ]
    for m in sent + back:
        m.wait_send()


def sems(*counts):
    out = []
    for n in counts:
        n = n if isinstance(n, tuple) else (n,)
        out += [pltpu.SemaphoreType.DMA(n), pltpu.SemaphoreType.DMA(n)]
    return out


def remote(number):
    return pltpu.CompilerParams(collective_id=number, has_side_effects=True, vmem_limit_bytes=LIMIT)


def shards(msa, pair, drop, w_bias, w_row, wo_row, w_col, wo_col, flanks, w_exit):
    seqs, length, width = msa.shape
    rows, _, depth = pair.shape
    wide = NY * NC - 1
    chunks = 2
    part = seqs // chunks * rows
    turned = pl.pallas_call(
        row_kernel,
        out_shape=jax.ShapeDtypeStruct((2, NX, NY * NC, chunks, part, LANES), BF16),
        in_specs=[VMEM] * 6,
        out_specs=VMEM,
        scratch_shapes=[
            pltpu.VMEM((2, rows * HEADS, LANES), BF16),
            pltpu.VMEM((2, NX, NY * NC, rows * HEADS, LANES), BF16),
            pltpu.VMEM((2, length * HEADS, LANES), F32),
            pltpu.VMEM((HEADS, length, length), F32),
            pltpu.VMEM((seqs, length, width), BF16),
            pltpu.VMEM((seqs, length, width), BF16),
            pltpu.VMEM((seqs, length, width), BF16),
            pltpu.VMEM((seqs, length, width), F32),
            pltpu.VMEM((seqs, HEADS, length, length), F32),
            pltpu.VMEM((2, length, LANES), F32),
            pltpu.VMEM((2, length // 2 * 8, LANES), F32),
            pltpu.VMEM((chunks, 2, NX, NY * NC, part, LANES), BF16),
            pltpu.VMEM((chunks, NX, NY * NC, part, LANES), BF16),
            pltpu.VMEM((chunks, NY * NC, NX, part, LANES), BF16),
            pltpu.SemaphoreType.DMA((2 * chunks,)),
        ]
        + sems(wide, wide, NX - 1, NY - 1, NX - 1, NY - 1)
        + sems((chunks, NX - 1), (chunks, wide), (chunks, wide), (chunks, NX - 1)),
        compiler_params=remote(0),
    )(pair.reshape(rows * length, depth), w_bias.T, msa, drop, w_row, wo_row)
    total = seqs * NX * NY * NC
    js = NX * rows
    lots = NY * rows * FACTORS // LANES
    per = LANES // FACTORS
    aligned, change = pl.pallas_call(
        column_kernel,
        out_shape=(
            jax.ShapeDtypeStruct((total * rows, width), BF16),
            jax.ShapeDtypeStruct(pair.shape, F32),
        ),
        in_specs=[VMEM] * 5,
        out_specs=(VMEM,) * 2,
        scratch_shapes=[
            pltpu.VMEM((2, total * rows, LANES), F32),
            pltpu.VMEM((total, width), BF16),
            pltpu.VMEM((total, width), BF16),
            pltpu.VMEM((total, width), BF16),
            pltpu.VMEM((total, width), F32),
            pltpu.VMEM((rows, FACTORS, total), BF16),
            pltpu.VMEM((rows, FACTORS, total), BF16),
            pltpu.VMEM((NY, rows, FACTORS, total), BF16),
            pltpu.VMEM((NX, rows, FACTORS, total), BF16),
            pltpu.VMEM((NX, rows, FACTORS, total), BF16),
            pltpu.VMEM((lots, 2 * js * (FACTORS + 8), LANES), F32),
            pltpu.VMEM(w_exit.shape, F32),
            pltpu.VMEM((FACTORS, LANES, per * depth), BF16),
            pltpu.VMEM((lots * 2 * js, FACTORS * LANES), BF16),
            pltpu.VMEM((NY, rows, 2 * js, depth), BF16),
            pltpu.VMEM((NY, rows, 2 * js, depth), BF16),
            pltpu.SemaphoreType.DMA((4,)),
        ]
        + sems((rows, NY - 1), (rows, NX - 1), (rows, NX), NY - 1),
        compiler_params=remote(1),
    )(turned, w_col, wo_col, flanks.T, w_exit)
    return aligned.reshape(total, rows, width), (pair.astype(F32) + change).astype(BF16)


def solution(mesh):
    torus = Mesh(mesh.devices.reshape(mesh.shape["groups"], NX, NY, NC), GROUPS_DAP)
    return jax.shard_map(
        shards,
        mesh=torus,
        in_specs=(
            P(GROUPS_DAP, None, None),
            P(GROUPS_DAP, None, None),
            P("groups", None),
        )
        + (P(),) * 7,
        out_specs=(P("groups", DAP, None), P(GROUPS_DAP, None, None)),
        check_vma=False,
    )
```

time: 132 us -> 91.6 us (0.69)
  Pallas kernels: 127 us -> 88 us
    pallas_call x4 -> x0, Pallas kernels: 96.2 us -> none  [the longest x1 39.7 us: shards(): pl.pallas_call(bias_gather_kernel, out_shape=jax.ShapeDtypeStruct((2, NX,...]
    pallas_call x1, Pallas kernels: 13.3 us -> 59.4 us  [shards(): pl.pallas_call(row_kernel, out_shape=jax.ShapeDtypeStruct((2, NX, NY * NC...]
    pallas_call x1, Pallas kernels: 17.5 us -> 28.6 us  [shards(): pl.pallas_call(column_kernel, out_shape=(jax.ShapeDtypeStruct((total * ro...]
where the time goes in v2:
time: 91.6 us; the launch traced here: 91.4 us
  Pallas kernels  88 us (96%)
  local copies, waits for them, and re-layouts  2.09 us (2%)
    pallas_call x1, Pallas kernels, shards(): pl.pallas_call(row_kernel, out_shape=jax.ShapeDtypeStruct((2, NX, NY * NC...  59.4 us
    pallas_call x1, Pallas kernels, shards(): pl.pallas_call(column_kernel, out_shape=(jax.ShapeDtypeStruct((total * ro...  28.6 us
    reshape x1, local copies, waits for them, and re-layouts, shards(): aligned.reshape(total, rows, width)  2.08 us

profile of v2, /device:TPU:513, one launch (start us, length us, event | category | flops | bytes accessed | tf_op | source)
XLA Modules:
  0.0 91.4 jit_solution(9642726724082661258)
XLA Ops:
  0.6 59.4 %shard_map.113.in_ref = bf16[2,8,16,2,4,128]{5,4,3,2,1,0:T(4,128)(2,1)} custom-call(bf16[512,128]{1,0:T(8,128)(2,1)} %bitcast.3, bf16[8,128]{1,0:T(8,128)(2,1)} %bitcast.5, bf16[4,256,256]{2,1,0:T(8,128)(2,1)} %msa_ref.1, s32[256,256]{1,0:T(8,128)} %drop_ref.1, bf16[256,1024]{1,0:T(8,128)(2,1)} %w_ref.2, bf16[256,256]{1,0:T(8,128)(2,1)} %wo_ref.2), custom_call_target="tpu_custom_call" | custom-call | tf_op jit(solution)/shard_map/pallas_call | solution.py:396
  60.0 28.6 %shard_map.114 = (bf16[1024,256]{1,0:T(8,128)(2,1)}, f32[2,256,128]{2,1,0:T(8,128)}) custom-call(bf16[2,8,16,2,4,128]{5,4,3,2,1,0:T(4,128)(2,1)} %shard_map.113.in_ref, bf16[256,1024]{1,0:T(8,128)(2,1)} %w_ref.3, bf16[256,256]{1,0:T(8,128)(2,1)} %wo_ref.3, bf16[64,256]{1,0:T(8,128)(2,1)} %bitcast.4, bf16[1024,128]{1,0:T(8,128)(2,1)} %exit_ref.1), custom_call_target="tpu_custom_call" | custom-call | tf_op jit(solution)/shard_map/pallas_call | solution.py:426
  88.6 0.0 copy-start
  88.6 0.0 copy-start.1
  88.6 2.1 %reshape.11 = bf16[512,2,256]{2,1,0:T(2,128)(2,1)} reshape(bf16[1024,256]{1,0:T(8,128)(2,1)} %get-tuple-element.4) | data formatting | bytes 1048576 | tf_op jit(solution)/shard_map/reshape | solution.py:456
  90.7 0.0 copy-done
  90.7 0.0 copy-done.1
  90.7 0.7 add_convert_fusion
Async XLA Ops:
  88.6 2.1 %copy-start = (bf16[2,256,128]{2,1,0:T(8,128)(2,1)S(1)}, bf16[2,256,128]{2,1,0:T(8,128)(2,1)}, u32[]{:S(2)}) copy-start(bf16[2,256,128]{2,1,0:T(8,128)(2,1)} %param.11) | copy-start | bytes 393220
  88.6 2.1 %copy-start.1 = (f32[2,256,128]{2,1,0:T(8,128)S(1)}, f32[2,256,128]{2,1,0:T(8,128)}, u32[]{:S(2)}) copy-start(f32[2,256,128]{2,1,0:T(8,128)} %get-tuple-element.5) | copy-start | bytes 786436

commit v3 on v2

--- a/solution.py
+++ b/solution.py
@@ -119,10 +119,14 @@
     return jnp.concatenate(tiles, axis=-1)
 
 
-def row_kernel(
-    pair_ref, wb_ref, msa_ref, drop_ref, w_ref, wo_ref, dst,
-    own, full, wide, bias, q, k, v, g, raw, res, stage, src, mid0, mid1, keep_sem,
-    s0, r0, s1, r1, s2, r2, s3, r3, s4, r4, s5, r5, e0, f0, e1, f1, e2, f2, e3, f3,
+def block_kernel(
+    pair_ref, wb_ref, flank_ref, msa_hbm, drop_hbm, w_row_hbm, wo_row_hbm, w_col_hbm, wo_col_hbm, exit_hbm,
+    out_ref, change,
+    msa_ref, drop_ref, w_ref, wo_ref, w_col, wo_col, exit_ref,
+    own, full, wide, bias, q, k, v, g, raw, res, stage, src, mid0, mid1, dst,
+    both, q2, k2, v2, g2, left, right, lefts, rights, others, prod, spread, diag, tile, arrive, land,
+    load_sem, keep_sem, s0, r0, s1, r1, s2, r2, s3, r3, s4, r4, s5, r5, e0, f0, e1, f1, e2, f2, e3, f3,
+    t0, u0, t1, u1, t2, u2, t3, u3,
 ):
     seqs, length, width = msa_ref.shape
     pairs = length // 2
@@ -130,6 +134,15 @@
     yc = y * NC + c
     wy, wx = wide_y(x, y, c), wide_x(x, y, c)
     count = knock([p for _, p, _, _ in wy] + [p for _, p, _, _ in wx[1:]])
+    loads = [
+        keep(a, b, load_sem.at[n])
+        for n, (a, b) in enumerate(
+            [
+                (msa_hbm, msa_ref), (w_row_hbm, w_ref), (drop_hbm, drop_ref), (wo_row_hbm, wo_ref),
+                (w_col_hbm, w_col), (wo_col_hbm, wo_col), (exit_hbm, exit_ref),
+            ]
+        )
+    ]
 
     zn = norm(pair_ref[...].astype(F32)).astype(BF16)
     rows = nt(wb_ref[...], zn)
@@ -141,6 +154,9 @@
     mine = [keep(own.at[t], full.at[t, x, yc], keep_sem.at[t]) for t in range(2)]
     first0 = [push(own.at[0], full.at[0, x, yc], s0.at[n], r0.at[n], p) for n, p, _, _ in wy]
     first1 = [push(own.at[1], full.at[1, x, yc], s1.at[n], r1.at[n], p) for n, p, _, _ in wx]
+
+    for m in loads:
+        m.wait()
 
     def project(s, carry):
         m1 = norm(msa_ref[s].astype(F32)).astype(BF16)
@@ -216,7 +232,7 @@
                     stage[t, pl.ds(i * 2 + r, pairs, stride=8), :] = res[t, pl.ds(r, pairs, stride=2), :]
             return carry
 
-        lax.fori_loop(0, group, one, 0)
+        lax.fori_loop(0, group, one, 0, unroll=2)
         for t in range(2):
             value = stage[t].reshape(NX, NY * NC, 8, LANES)[:, :, : group * 2, :]
             src[n, t] = value.astype(BF16)
@@ -255,64 +271,50 @@
         b.wait()
         for m in g0 + g1:
             m.wait_recv()
-    for m in sent:
-        m.wait_send()
-
-
-def column_kernel(
-    in_ref, w_ref, wo_ref, flank_ref, exit_ref, out_ref, change,
-    both, q, k, v, g, left, right, lefts, rights, others, prod, wide, diag, tile, arrive, land,
-    keep_sem, s0, r0, s1, r1, s2, r2, s3, r3,
-):
-    width = w_ref.shape[0]
-    tokens = out_ref.shape[0]
-    seqs = tokens // 2
-    x, y, c = here()
-    other = place(x, y, 1 - c)
-    count = knock(y_peers(x, y, c) + x_peers(x, y, c) + [other])
+
+
+    seqs, tokens = out_ref.shape[0], 2 * out_ref.shape[0]
     for t in range(2):
-        both[t] = in_ref[t].astype(F32).reshape(tokens, LANES)
-    sent, moves = [], []
+        both[t] = dst[t].astype(F32).reshape(tokens, LANES)
+    moves = []
     for r in range(2):
         token = jnp.concatenate([both[t, pl.ds(r, seqs, stride=2), :] for t in range(2)], axis=-1)
         m3 = norm(token).astype(BF16)
-        q[...] = (nn(m3, w_ref[:, 0:width]) * WIDTH ** (-0.5)).astype(BF16)
-        k[...] = nn(m3, w_ref[:, width : 2 * width]).astype(BF16)
-        v[...] = nn(m3, w_ref[:, 2 * width : 3 * width]).astype(BF16)
-        g[...] = nn(m3, w_ref[:, 3 * width : 4 * width])
+        q2[...] = (nn(m3, w_col[:, 0:width]) * WIDTH ** (-0.5)).astype(BF16)
+        k2[...] = nn(m3, w_col[:, width : 2 * width]).astype(BF16)
+        v2[...] = nn(m3, w_col[:, 2 * width : 3 * width]).astype(BF16)
+        g2[...] = nn(m3, w_col[:, 3 * width : 4 * width])
         parts = []
         for h in range(HEADS):
             part, mask = head(h)
-            parts.append(softmax_product(nt(q[:, part] * mask, k[:, part]), v[:, part] * mask))
-        gated = (jax.nn.sigmoid(g[...]) * merge(parts)).astype(BF16)
-        after = (token + nn(gated, wo_ref[...])).astype(BF16).astype(F32)
+            parts.append(softmax_product(nt(q2[:, part] * mask, k2[:, part]), v2[:, part] * mask))
+        gated = (jax.nn.sigmoid(g2[...]) * merge(parts)).astype(BF16)
+        after = (token + nn(gated, wo_col[...])).astype(BF16).astype(F32)
         for t in range(2):
             both[t, pl.ds(r, seqs, stride=2), :] = after[:, t * LANES : (t + 1) * LANES]
         factors = nt(flank_ref[...], norm(after).astype(BF16)).astype(BF16)
         left[r] = factors[:FACTORS]
         right[r] = factors[FACTORS:]
-        if r == 0:
-            answered(count)
         own = [keep(left.at[r], lefts.at[y, r], keep_sem.at[2 * r]), keep(right.at[r], rights.at[x, r], keep_sem.at[2 * r + 1])]
         fl = [
-            push(left.at[r], lefts.at[y, r], s0.at[r, d - 1], r0.at[r, d - 1], place(x, (y + d) % NY, c))
+            push(left.at[r], lefts.at[y, r], t0.at[r, d - 1], u0.at[r, d - 1], place(x, (y + d) % NY, c))
             for d in RING_ORDER
         ]
         fr = [
-            push(right.at[r], rights.at[x, r], s1.at[r, d - 1], r1.at[r, d - 1], place((x + d) % NX, y, c))
+            push(right.at[r], rights.at[x, r], t1.at[r, d - 1], u1.at[r, d - 1], place((x + d) % NX, y, c))
             for d in RING_ORDER
         ]
-        swap = [push(right.at[r], others.at[x, r], s2.at[r, NX - 1], r2.at[r, NX - 1], other)]
+        swap = [push(right.at[r], others.at[x, r], t2.at[r, NX - 1], u2.at[r, NX - 1], other)]
         moves.append((own, fl, fr, swap))
 
     for t in range(2):
-        out_ref[:, t * LANES : (t + 1) * LANES] = both[t].astype(BF16)
+        out_ref[:, t] = both[t].reshape(seqs, 2, LANES).astype(BF16)
     depth = exit_ref.shape[1]
     per = LANES // FACTORS
-    wide[...] = exit_ref[...].astype(F32)
+    spread[...] = exit_ref[...].astype(F32)
     diag[...] = jnp.zeros_like(diag)
     for d in range(FACTORS):
-        block = wide[pl.ds(d, FACTORS, stride=FACTORS), :].astype(BF16)
+        block = spread[pl.ds(d, FACTORS, stride=FACTORS), :].astype(BF16)
         for e in range(per):
             diag[d, e * FACTORS : (e + 1) * FACTORS, e * depth : (e + 1) * depth] = block
 
@@ -321,7 +323,7 @@
             d = RING_ORDER[n]
             fr[n].wait_recv()
             xs = (x + NX - d) % NX
-            swap.append(push(rights.at[xs, r], others.at[xs, r], s2.at[r, d - 1], r2.at[r, d - 1], other))
+            swap.append(push(rights.at[xs, r], others.at[xs, r], t2.at[r, d - 1], u2.at[r, d - 1], other))
         for m in own:
             m.wait()
         for m in fl:
@@ -357,7 +359,7 @@
             arrive[i // 2, i % 2] = update[u * 2 * js : (u + 1) * 2 * js, e * depth : (e + 1) * depth].astype(BF16)
     own = keep(arrive.at[y], land.at[y], keep_sem.at[0])
     back = [
-        push(arrive.at[(y + d) % NY], land.at[y], s3.at[d - 1], r3.at[d - 1], place(x, (y + d) % NY, c))
+        push(arrive.at[(y + d) % NY], land.at[y], t3.at[d - 1], u3.at[d - 1], place(x, (y + d) % NY, c))
         for d in RING_ORDER
     ]
     own.wait()
@@ -393,12 +395,21 @@
     wide = NY * NC - 1
     chunks = 2
     part = seqs // chunks * rows
-    turned = pl.pallas_call(
-        row_kernel,
-        out_shape=jax.ShapeDtypeStruct((2, NX, NY * NC, chunks, part, LANES), BF16),
-        in_specs=[VMEM] * 6,
-        out_specs=VMEM,
-        scratch_shapes=[
+    total = seqs * NX * NY * NC
+    js = NX * rows
+    lots = NY * rows * FACTORS // LANES
+    per = LANES // FACTORS
+    later = (msa, drop, w_row, wo_row, w_col, wo_col, w_exit)
+    aligned, change = pl.pallas_call(
+        block_kernel,
+        out_shape=(
+            jax.ShapeDtypeStruct((total, width // LANES, rows, LANES), BF16),
+            jax.ShapeDtypeStruct(pair.shape, F32),
+        ),
+        in_specs=[VMEM] * 3 + [pl.BlockSpec(memory_space=pl.ANY)] * len(later),
+        out_specs=(VMEM,) * 2,
+        scratch_shapes=[pltpu.VMEM(a.shape, a.dtype) for a in later]
+        + [
             pltpu.VMEM((2, rows * HEADS, LANES), BF16),
             pltpu.VMEM((2, NX, NY * NC, rows * HEADS, LANES), BF16),
             pltpu.VMEM((2, length * HEADS, LANES), F32),
@@ -413,25 +424,7 @@
             pltpu.VMEM((chunks, 2, NX, NY * NC, part, LANES), BF16),
             pltpu.VMEM((chunks, NX, NY * NC, part, LANES), BF16),
             pltpu.VMEM((chunks, NY * NC, NX, part, LANES), BF16),
-            pltpu.SemaphoreType.DMA((2 * chunks,)),
-        ]
-        + sems(wide, wide, NX - 1, NY - 1, NX - 1, NY - 1)
-        + sems((chunks, NX - 1), (chunks, wide), (chunks, wide), (chunks, NX - 1)),
-        compiler_params=remote(0),
-    )(pair.reshape(rows * length, depth), w_bias.T, msa, drop, w_row, wo_row)
-    total = seqs * NX * NY * NC
-    js = NX * rows
-    lots = NY * rows * FACTORS // LANES
-    per = LANES // FACTORS
-    aligned, change = pl.pallas_call(
-        column_kernel,
-        out_shape=(
-            jax.ShapeDtypeStruct((total * rows, width), BF16),
-            jax.ShapeDtypeStruct(pair.shape, F32),
-        ),
-        in_specs=[VMEM] * 5,
-        out_specs=(VMEM,) * 2,
-        scratch_shapes=[
+            pltpu.VMEM((2, NX, NY * NC, chunks, part, LANES), BF16),
             pltpu.VMEM((2, total * rows, LANES), F32),
             pltpu.VMEM((total, width), BF16),
             pltpu.VMEM((total, width), BF16),
@@ -448,12 +441,15 @@
             pltpu.VMEM((lots * 2 * js, FACTORS * LANES), BF16),
             pltpu.VMEM((NY, rows, 2 * js, depth), BF16),
             pltpu.VMEM((NY, rows, 2 * js, depth), BF16),
-            pltpu.SemaphoreType.DMA((4,)),
-        ]
+            pltpu.SemaphoreType.DMA((len(later),)),
+            pltpu.SemaphoreType.DMA((2 * chunks,)),
+        ]
+        + sems(wide, wide, NX - 1, NY - 1, NX - 1, NY - 1)
+        + sems((chunks, NX - 1), (chunks, wide), (chunks, wide), (chunks, NX - 1))
         + sems((rows, NY - 1), (rows, NX - 1), (rows, NX), NY - 1),
-        compiler_params=remote(1),
-    )(turned, w_col, wo_col, flanks.T, w_exit)
-    return aligned.reshape(total, rows, width), (pair.astype(F32) + change).astype(BF16)
+        compiler_params=remote(0),
+    )(pair.reshape(rows * length, depth), w_bias.T, flanks.T, *later)
+    return aligned.transpose(0, 2, 1, 3).reshape(total, rows, width), (pair.astype(F32) + change).astype(BF16)
 
 
 def solution(mesh):

time: 91.6 us -> 88.5 us (0.966)
  Pallas kernels: 88 us -> 85.1 us
  local copies, waits for them, and re-layouts: 2.09 us -> 0.8 us
  other arithmetic: 0.68 us -> 1.69 us
    pallas_call x2 -> x1, Pallas kernels: 88 us -> 85.1 us  [shards(): pl.pallas_call(block_kernel, out_shape=(jax.ShapeDtypeStruct((total, widt...]
    reshape x1 -> x0, local copies, waits for them, and re-layouts: 2.08 us -> none  [shards(): aligned.reshape(total, rows, width)]
    convert_element_type x1, other arithmetic: 0.68 us -> 1.69 us  [shards(): (pair.astype(F32) + change).astype(BF16)]
where the time goes in v3:
time: 88.5 us; the launch traced here: 88.3 us
  Pallas kernels  85.1 us (96%)
  other arithmetic  1.69 us (2%)
    pallas_call x1, Pallas kernels, shards(): pl.pallas_call(block_kernel, out_shape=(jax.ShapeDtypeStruct((total, widt...  85.1 us

profile of v3, /device:TPU:513, one launch (start us, length us, event | category | flops | bytes accessed | tf_op | source)
XLA Modules:
  0.0 88.3 jit_solution(15677638201519989140)
XLA Ops:
  0.6 0.0 copy-start.1
  0.6 85.1 %shard_map.113 = (bf16[512,2,2,128]{3,2,1,0:T(2,128)(2,1)}, f32[2,256,128]{2,1,0:T(8,128)}) custom-call(bf16[512,128]{1,0:T(8,128)(2,1)} %bitcast.7, bf16[8,128]{1,0:T(8,128)(2,1)} %bitcast.9, bf16[64,256]{1,0:T(8,128)(2,1)} %bitcast.8, bf16[4,256,256]{2,1,0:T(8,128)(2,1)} %msa_hbm.1, s32[256,256]{1,0:T(8,128)} %drop_hbm.1, bf16[256,1024]{1,0:T(8,128)(2,1)} %w_row_hbm.1, ...), custom_call_target="tpu_custom_call" | custom-call | tf_op jit(solution)/shard_map/pallas_call | solution.py:403
  85.8 0.0 copy-start
  85.8 0.0 copy-done.1
  85.8 1.7 %add_convert_fusion = bf16[2,256,128]{2,1,0:T(8,128)(2,1)} fusion(f32[2,256,128]{2,1,0:T(8,128)} %get-tuple-element.5, bf16[2,256,128]{2,1,0:T(8,128)(2,1)S(1)} %copy-done.1), kind=kLoop, calls=%fused_computation | loop fusion | flops 196608 | bytes 524288 | tf_op jit(solution)/shard_map/convert_element_type | solution.py:452
  87.5 0.0 copy-done
  87.5 0.8 copy.13
Async XLA Ops:
  0.6 85.2 %copy-start.1 = (bf16[2,256,128]{2,1,0:T(8,128)(2,1)S(1)}, bf16[2,256,128]{2,1,0:T(8,128)(2,1)}, u32[]{:S(2)}) copy-start(bf16[2,256,128]{2,1,0:T(8,128)(2,1)} %param.11) | copy-start | bytes 393220
  85.8 1.7 %copy-start = (bf16[512,2,2,128]{3,2,1,0:T(2,128)(2,1)S(1)}, bf16[512,2,2,128]{3,2,1,0:T(2,128)(2,1)}, u32[]{:S(2)}) copy-start(bf16[512,2,2,128]{3,2,1,0:T(2,128)(2,1)} %get-tuple-element.4) | copy-start | bytes 1572868

commit v4 on v3

--- a/solution.py
+++ b/solution.py
@@ -75,6 +75,31 @@
     return copy
 
 
+def near(source, view, me, peer, send, recv):
+    return {d: push(source, view(me), send(d - 1), recv(d - 1), peer(d)) for d in (2, 6, 1, 7)}
+
+
+def far(view, me, peer, send, recv, sent):
+    back, ahead = (me + 6) % 8, (me + 2) % 8
+    sent[2].wait_recv()
+    out = {4: push(view(back, 0), view(back, 0), send(3), recv(3), peer(2))}
+    out[3] = push(view(back), view(back), send(2), recv(2), peer(1))
+    sent[6].wait_recv()
+    out[8] = push(view(ahead, 1), view(ahead, 1), send(7), recv(7), peer(6))
+    out[5] = push(view(ahead), view(ahead), send(4), recv(4), peer(7))
+    return out
+
+
+def landed(sent, onward, d):
+    if d in (1, 7):
+        sent[d].wait_recv()
+    elif d in (3, 5):
+        onward[d].wait_recv()
+    elif d == 4:
+        onward[4].wait_recv()
+        onward[8].wait_recv()
+
+
 def wide_y(x, y, c):
     out = [(NY * NC - 2, place(x, y, 1 - c), y, 1 - c)]
     for k in RING_ORDER:
@@ -124,7 +149,7 @@
     out_ref, change,
     msa_ref, drop_ref, w_ref, wo_ref, w_col, wo_col, exit_ref,
     own, full, wide, bias, q, k, v, g, raw, res, stage, src, mid0, mid1, dst,
-    both, q2, k2, v2, g2, left, right, lefts, rights, others, prod, spread, diag, tile, arrive, land,
+    both, q2, k2, v2, g2, left, right, lefts, rights, others, prod, spread, diag, tile, arrive, land, total,
     load_sem, keep_sem, s0, r0, s1, r1, s2, r2, s3, r3, s4, r4, s5, r5, e0, f0, e1, f1, e2, f2, e3, f3,
     t0, u0, t1, u1, t2, u2, t3, u3,
 ):
@@ -171,18 +196,25 @@
         m.wait()
     for m in first0:
         m.wait_recv()
-    half = pl.ds(c * NY, NY)
-    second0 = [
-        push(full.at[0, x, half], full.at[0, x, half], s2.at[n - 1], r2.at[n - 1], place((x + n) % NX, y, c))
-        for n in RING_ORDER
-    ]
+
+    def ring_x(at, part=None):
+        at_y = pl.ds(c * NY, NY) if part is None else pl.ds(c * NY + part * (NY // 2), NY // 2)
+        return full.at[0, at, at_y]
+
+    def ring_y(at, part=None):
+        at_x = pl.ds(c * (NX // 2), NX // 2) if part is None else pl.ds(c * (NX // 2) + part * (NX // 4), NX // 4)
+        return full.at[1, at_x, pl.ds(at * NC, NC)]
+
+    def to_x(d):
+        return place((x + d) % NX, y, c)
+
+    def to_y(d):
+        return place(x, (y + d) % NY, c)
+
+    second0 = near(ring_x(x), ring_x, x, to_x, lambda n: s2.at[n], lambda n: r2.at[n])
     for m in first1:
         m.wait_recv()
-    halfx, pair = pl.ds(c * (NX // 2), NX // 2), pl.ds(y * NC, NC)
-    second1 = [
-        push(full.at[1, halfx, pair], full.at[1, halfx, pair], s3.at[n - 1], r3.at[n - 1], place(x, (y + n) % NY, c))
-        for n in RING_ORDER
-    ]
+    second1 = near(ring_y(y), ring_y, y, to_y, lambda n: s3.at[n], lambda n: r3.at[n])
 
     def score(s, carry):
         for h in range(HEADS):
@@ -193,16 +225,15 @@
     lax.fori_loop(0, seqs, score, 0)
     other = place(x, y, 1 - c)
     third = []
-    for n in reversed(range(NX - 1)):
-        d = RING_ORDER[n]
-        second0[n].wait_recv()
-        xs = (x + NX - d) % NX
-        third.append(push(full.at[0, xs, half], full.at[0, xs, half], s4.at[d - 1], r4.at[d - 1], other))
-        second1[n].wait_recv()
-        pairs_of = pl.ds(((y + NY - d) % NY) * NC, NC)
-        third.append(
-            push(full.at[1, halfx, pairs_of], full.at[1, halfx, pairs_of], s5.at[d - 1], r5.at[d - 1], other)
-        )
+    onward0 = far(ring_x, x, to_x, lambda n: s2.at[n], lambda n: r2.at[n], second0)
+    onward1 = far(ring_y, y, to_y, lambda n: s3.at[n], lambda n: r3.at[n], second1)
+    for d in (2, 6, 1, 7, 3, 5, 4):
+        landed(second0, onward0, d)
+        block = ring_x((x + NX - d) % NX)
+        third.append(push(block, block, s4.at[d - 1], r4.at[d - 1], other))
+        landed(second1, onward1, d)
+        block = ring_y((y + NY - d) % NY)
+        third.append(push(block, block, s5.at[d - 1], r5.at[d - 1], other))
     for m in third:
         m.wait_recv()
     for t in range(2):
@@ -213,7 +244,9 @@
 
     chunks = src.shape[0]
     group = seqs // chunks
-    sent = first0 + first1 + second0 + second1 + third
+    sent = first0 + first1 + third
+    for some in (second0, onward0, second1, onward1):
+        sent += list(some.values())
     hops = []
     for n in range(chunks):
 
@@ -277,6 +310,15 @@
     for t in range(2):
         both[t] = dst[t].astype(F32).reshape(tokens, LANES)
     moves = []
+
+    def factor_view(ref, r):
+        def view(at, part=None):
+            if part is None:
+                return ref.at[at, r]
+            return ref.at[at, r, pl.ds(part * (FACTORS // 2), FACTORS // 2)]
+
+        return view
+
     for r in range(2):
         token = jnp.concatenate([both[t, pl.ds(r, seqs, stride=2), :] for t in range(2)], axis=-1)
         m3 = norm(token).astype(BF16)
@@ -296,17 +338,27 @@
         left[r] = factors[:FACTORS]
         right[r] = factors[FACTORS:]
         own = [keep(left.at[r], lefts.at[y, r], keep_sem.at[2 * r]), keep(right.at[r], rights.at[x, r], keep_sem.at[2 * r + 1])]
-        fl = [
-            push(left.at[r], lefts.at[y, r], t0.at[r, d - 1], u0.at[r, d - 1], place(x, (y + d) % NY, c))
-            for d in RING_ORDER
-        ]
-        fr = [
-            push(right.at[r], rights.at[x, r], t1.at[r, d - 1], u1.at[r, d - 1], place((x + d) % NX, y, c))
-            for d in RING_ORDER
-        ]
         swap = [push(right.at[r], others.at[x, r], t2.at[r, NX - 1], u2.at[r, NX - 1], other)]
-        moves.append((own, fl, fr, swap))
-
+        ways = (factor_view(lefts, r), factor_view(rights, r))
+        sems_l = (lambda n, r=r: t0.at[r, n], lambda n, r=r: u0.at[r, n])
+        sems_r = (lambda n, r=r: t1.at[r, n], lambda n, r=r: u1.at[r, n])
+        fl = near(left.at[r], ways[0], y, to_y, *sems_l)
+        fr = near(right.at[r], ways[1], x, to_x, *sems_r)
+        moves.append((own, fl, fr, swap, ways, sems_l, sems_r))
+
+    def forward(r):
+        _, fl, fr, _, ways, sems_l, sems_r = moves[r]
+        return far(ways[0], y, to_y, *sems_l, fl), far(ways[1], x, to_x, *sems_r, fr)
+
+    def hand(r, onward, ds):
+        _, fl, fr, swap, _, _, _ = moves[r]
+        for d in ds:
+            landed(fr, onward[1], d)
+            xs = (x + NX - d) % NX
+            swap.append(push(rights.at[xs, r], others.at[xs, r], t2.at[r, d - 1], u2.at[r, d - 1], other))
+            landed(fl, onward[0], d)
+
+    ahead0 = forward(0)
     for t in range(2):
         out_ref[:, t] = both[t].reshape(seqs, 2, LANES).astype(BF16)
     depth = exit_ref.shape[1]
@@ -318,17 +370,18 @@
         for e in range(per):
             diag[d, e * FACTORS : (e + 1) * FACTORS, e * depth : (e + 1) * depth] = block
 
-    for r, (own, fl, fr, swap) in enumerate(moves):
-        for n in reversed(range(NX - 1)):
-            d = RING_ORDER[n]
-            fr[n].wait_recv()
-            xs = (x + NX - d) % NX
-            swap.append(push(rights.at[xs, r], others.at[xs, r], t2.at[r, d - 1], u2.at[r, d - 1], other))
+    hand(0, ahead0, (2, 6, 1, 7))
+    ahead1 = forward(1)
+    hand(1, ahead1, (2, 6, 1, 7))
+    hand(0, ahead0, (3, 5, 4))
+    hand(1, ahead1, (3, 5, 4))
+    for own, fl, fr, swap, _, _, _ in moves:
         for m in own:
             m.wait()
-        for m in fl:
-            m.wait_recv()
-        sent += fl + fr + swap
+        sent += list(fl.values()) + list(fr.values()) + swap
+    for ways in (ahead0, ahead1):
+        for some in ways:
+            sent += list(some.values())
 
     rows = rights.shape[0] * rights.shape[1] * rights.shape[2]
     js = rows // FACTORS
@@ -344,8 +397,8 @@
                 prod[u, at, :] = out[n * FACTORS : (n + 1) * FACTORS, u * LANES : (u + 1) * LANES]
 
     fill(rights, c * js)
-    for _, _, _, swap in moves:
-        for m in swap:
+    for move in moves:
+        for m in move[3]:
             m.wait_recv()
     fill(others, (1 - c) * js)
     for d in range(FACTORS):
@@ -370,9 +423,11 @@
             prod[t, yy * 2 * js : (yy + 1) * 2 * js, :] = land[yy, t].astype(F32)
             for cc in range(NC):
                 for r in range(2):
-                    change[t, pl.ds((yy * NC + cc) * 2 + r, NX, stride=NY * NC * 2), :] = prod[
+                    total[t, pl.ds((yy * NC + cc) * 2 + r, NX, stride=NY * NC * 2), :] = prod[
                         t, pl.ds(yy * 2 * js + cc * js + r, NX, stride=2), :
                     ]
+        here_pair = pair_ref[t * length : (t + 1) * length, :].astype(F32)
+        change[t] = (here_pair + total[t]).astype(BF16)
     for m in sent + back:
         m.wait_send()
 
@@ -400,11 +455,11 @@
     lots = NY * rows * FACTORS // LANES
     per = LANES // FACTORS
     later = (msa, drop, w_row, wo_row, w_col, wo_col, w_exit)
-    aligned, change = pl.pallas_call(
+    aligned, pair_after = pl.pallas_call(
         block_kernel,
         out_shape=(
             jax.ShapeDtypeStruct((total, width // LANES, rows, LANES), BF16),
-            jax.ShapeDtypeStruct(pair.shape, F32),
+            jax.ShapeDtypeStruct(pair.shape, BF16),
         ),
         in_specs=[VMEM] * 3 + [pl.BlockSpec(memory_space=pl.ANY)] * len(later),
         out_specs=(VMEM,) * 2,
@@ -441,15 +496,16 @@
             pltpu.VMEM((lots * 2 * js, FACTORS * LANES), BF16),
             pltpu.VMEM((NY, rows, 2 * js, depth), BF16),
             pltpu.VMEM((NY, rows, 2 * js, depth), BF16),
+            pltpu.VMEM(pair.shape, F32),
             pltpu.SemaphoreType.DMA((len(later),)),
             pltpu.SemaphoreType.DMA((2 * chunks,)),
         ]
-        + sems(wide, wide, NX - 1, NY - 1, NX - 1, NY - 1)
+        + sems(wide, wide, NX, NY, NX - 1, NY - 1)
         + sems((chunks, NX - 1), (chunks, wide), (chunks, wide), (chunks, NX - 1))
-        + sems((rows, NY - 1), (rows, NX - 1), (rows, NX), NY - 1),
+        + sems((rows, NY), (rows, NX), (rows, NX), NY - 1),
         compiler_params=remote(0),
     )(pair.reshape(rows * length, depth), w_bias.T, flanks.T, *later)
-    return aligned.transpose(0, 2, 1, 3).reshape(total, rows, width), (pair.astype(F32) + change).astype(BF16)
+    return aligned.transpose(0, 2, 1, 3).reshape(total, rows, width), pair_after
 
 
 def solution(mesh):

time: 88.5 us -> 87.4 us (0.988)
  local copies, waits for them, and re-layouts: 0.8 us -> 2.89 us
  other arithmetic: 1.69 us -> 0 us
  Pallas kernels: 85.1 us -> 83.7 us
    unnamed x5 -> x4, local copies, waits for them, and re-layouts: 0.8 us -> 2.89 us
    convert_element_type x1 -> x0, other arithmetic: 1.69 us -> none  [shards(): (pair.astype(F32) + change).astype(BF16)]
    pallas_call x1, Pallas kernels: 85.1 us -> 83.7 us  [shards(): pl.pallas_call(block_kernel, out_shape=(jax.ShapeDtypeStruct((total, widt...]
where the time goes in v4:
time: 87.4 us; the launch traced here: 87.2 us
  Pallas kernels  83.7 us (96%)
  local copies, waits for them, and re-layouts  2.89 us (3%)
    pallas_call x1, Pallas kernels, shards(): pl.pallas_call(block_kernel, out_shape=(jax.ShapeDtypeStruct((total, widt...  83.7 us
    unnamed x4, local copies, waits for them, and re-layouts  2.89 us

profile of v4, /device:TPU:513, one launch (start us, length us, event | category | flops | bytes accessed | tf_op | source)
XLA Modules:
  0.0 87.2 jit_solution(17826854267311649754)
XLA Ops:
  0.6 83.7 %shard_map.113 = (bf16[512,2,2,128]{3,2,1,0:T(2,128)(2,1)}, bf16[2,256,128]{2,1,0:T(8,128)(2,1)}) custom-call(bf16[512,128]{1,0:T(8,128)(2,1)} %bitcast.7, bf16[8,128]{1,0:T(8,128)(2,1)} %bitcast.9, bf16[64,256]{1,0:T(8,128)(2,1)} %bitcast.8, bf16[4,256,256]{2,1,0:T(8,128)(2,1)} %msa_hbm.1, s32[256,256]{1,0:T(8,128)} %drop_hbm.1, ...), custom_call_target="tpu_custom_call" | custom-call | tf_op jit(solution)/shard_map/pallas_call | solution.py:458
  84.3 0.0 copy-start
  84.3 2.2 %copy.14 = bf16[512,2,256]{2,1,0:T(2,128)(2,1)} copy(bf16[512,2,256]{2,1,0:T(2,128)(2,1)} %bitcast.6) | data formatting | bytes 1048576
  86.6 0.0 copy-done
  86.6 0.7 copy.15
Async XLA Ops:
  84.3 2.2 %copy-start = (bf16[2,256,128]{2,1,0:T(8,128)(2,1)S(1)}, bf16[2,256,128]{2,1,0:T(8,128)(2,1)}, u32[]{:S(2)}) copy-start(bf16[2,256,128]{2,1,0:T(8,128)(2,1)} %get-tuple-element.9) | copy-start | bytes 393220

commit v5 on v4

--- a/solution.py
+++ b/solution.py
@@ -145,9 +145,9 @@
 
 
 def block_kernel(
-    pair_ref, wb_ref, flank_ref, msa_hbm, drop_hbm, w_row_hbm, wo_row_hbm, w_col_hbm, wo_col_hbm, exit_hbm,
+    pair_hbm, wb_hbm, flank_hbm, msa_hbm, drop_hbm, w_row_hbm, wo_row_hbm, w_col_hbm, wo_col_hbm, exit_hbm,
     out_ref, change,
-    msa_ref, drop_ref, w_ref, wo_ref, w_col, wo_col, exit_ref,
+    pair_ref, wb_ref, flank_ref, msa_ref, drop_ref, w_ref, wo_ref, w_col, wo_col, exit_ref,
     own, full, wide, bias, q, k, v, g, raw, res, stage, src, mid0, mid1, dst,
     both, q2, k2, v2, g2, left, right, lefts, rights, others, prod, spread, diag, tile, arrive, land, total,
     load_sem, keep_sem, s0, r0, s1, r1, s2, r2, s3, r3, s4, r4, s5, r5, e0, f0, e1, f1, e2, f2, e3, f3,
@@ -163,12 +163,14 @@
         keep(a, b, load_sem.at[n])
         for n, (a, b) in enumerate(
             [
-                (msa_hbm, msa_ref), (w_row_hbm, w_ref), (drop_hbm, drop_ref), (wo_row_hbm, wo_ref),
+                (pair_hbm, pair_ref), (wb_hbm, wb_ref), (flank_hbm, flank_ref), (msa_hbm, msa_ref), (w_row_hbm, w_ref), (drop_hbm, drop_ref), (wo_row_hbm, wo_ref),
                 (w_col_hbm, w_col), (wo_col_hbm, wo_col), (exit_hbm, exit_ref),
             ]
         )
     ]
 
+    for m in loads[:2]:
+        m.wait()
     zn = norm(pair_ref[...].astype(F32)).astype(BF16)
     rows = nt(wb_ref[...], zn)
     rows = jnp.concatenate([rows[:, :length], rows[:, length:]], axis=0).astype(BF16)
@@ -180,7 +182,7 @@
     first0 = [push(own.at[0], full.at[0, x, yc], s0.at[n], r0.at[n], p) for n, p, _, _ in wy]
     first1 = [push(own.at[1], full.at[1, x, yc], s1.at[n], r1.at[n], p) for n, p, _, _ in wx]
 
-    for m in loads:
+    for m in loads[2:]:
         m.wait()
 
     def project(s, carry):
@@ -389,42 +391,46 @@
     cols = lefts[...].reshape(rows, seqs)
     lots = rows // LANES
 
-    def fill(source, base):
+    back = []
+    own = []
+
+    def update(n, source, slot):
         out = nt(source[...].reshape(rows, seqs), cols) * (1.0 / seqs)
-        for n in range(js):
+        for j in range(js):
             for u in range(lots):
-                at = pl.ds(pl.multiple_of((base + n) * pitch, 8), FACTORS)
-                prod[u, at, :] = out[n * FACTORS : (n + 1) * FACTORS, u * LANES : (u + 1) * LANES]
-
-    fill(rights, c * js)
+                prod[u, j * pitch : j * pitch + FACTORS, :] = out[
+                    j * FACTORS : (j + 1) * FACTORS, u * LANES : (u + 1) * LANES
+                ]
+        for d in range(FACTORS):
+            tile[:, d * LANES : (d + 1) * LANES] = jnp.concatenate(
+                [prod[u, pl.ds(d, js, stride=pitch), :] for u in range(lots)], axis=0
+            ).astype(BF16)
+        add = nn(tile[...], diag[...].reshape(FACTORS * LANES, per * depth))
+        for u in range(lots):
+            for e in range(per):
+                i = u * per + e
+                arrive[n, i // 2, i % 2] = add[u * js : (u + 1) * js, e * depth : (e + 1) * depth].astype(BF16)
+        own.append(keep(arrive.at[n, y], land.at[slot, y], keep_sem.at[n]))
+        for d in RING_ORDER:
+            back.append(push(arrive.at[n, (y + d) % NY], land.at[slot, y], t3.at[n, d - 1], u3.at[n, d - 1], to_y(d)))
+
+    update(0, rights, c)
     for move in moves:
         for m in move[3]:
             m.wait_recv()
-    fill(others, (1 - c) * js)
-    for d in range(FACTORS):
-        tile[:, d * LANES : (d + 1) * LANES] = jnp.concatenate(
-            [prod[u, pl.ds(d, 2 * js, stride=pitch), :] for u in range(lots)], axis=0
-        ).astype(BF16)
-    update = nn(tile[...], diag[...].reshape(FACTORS * LANES, per * depth))
-    for u in range(lots):
-        for e in range(per):
-            i = u * per + e
-            arrive[i // 2, i % 2] = update[u * 2 * js : (u + 1) * 2 * js, e * depth : (e + 1) * depth].astype(BF16)
-    own = keep(arrive.at[y], land.at[y], keep_sem.at[0])
-    back = [
-        push(arrive.at[(y + d) % NY], land.at[y], t3.at[d - 1], u3.at[d - 1], place(x, (y + d) % NY, c))
-        for d in RING_ORDER
-    ]
-    own.wait()
+    update(1, others, 1 - c)
+    for m in own:
+        m.wait()
     for m in back:
         m.wait_recv()
     for t in range(2):
         for yy in range(NY):
-            prod[t, yy * 2 * js : (yy + 1) * 2 * js, :] = land[yy, t].astype(F32)
             for cc in range(NC):
+                base = (yy * NC + cc) * js
+                prod[t, base : base + js, :] = land[cc, yy, t].astype(F32)
                 for r in range(2):
                     total[t, pl.ds((yy * NC + cc) * 2 + r, NX, stride=NY * NC * 2), :] = prod[
-                        t, pl.ds(yy * 2 * js + cc * js + r, NX, stride=2), :
+                        t, pl.ds(base + r, NX, stride=2), :
                     ]
         here_pair = pair_ref[t * length : (t + 1) * length, :].astype(F32)
         change[t] = (here_pair + total[t]).astype(BF16)
@@ -454,14 +460,14 @@
     js = NX * rows
     lots = NY * rows * FACTORS // LANES
     per = LANES // FACTORS
-    later = (msa, drop, w_row, wo_row, w_col, wo_col, w_exit)
+    later = (pair.reshape(rows * length, depth), w_bias.T, flanks.T, msa, drop, w_row, wo_row, w_col, wo_col, w_exit)
     aligned, pair_after = pl.pallas_call(
         block_kernel,
         out_shape=(
-            jax.ShapeDtypeStruct((total, width // LANES, rows, LANES), BF16),
-            jax.ShapeDtypeStruct(pair.shape, BF16),
+            pltpu.VMEM((total, width // LANES, rows, LANES), BF16),
+            pltpu.VMEM(pair.shape, BF16),
         ),
-        in_specs=[VMEM] * 3 + [pl.BlockSpec(memory_space=pl.ANY)] * len(later),
+        in_specs=[pl.BlockSpec(memory_space=pl.ANY)] * len(later),
         out_specs=(VMEM,) * 2,
         scratch_shapes=[pltpu.VMEM(a.shape, a.dtype) for a in later]
         + [
@@ -490,21 +496,21 @@
             pltpu.VMEM((NY, rows, FACTORS, total), BF16),
             pltpu.VMEM((NX, rows, FACTORS, total), BF16),
             pltpu.VMEM((NX, rows, FACTORS, total), BF16),
-            pltpu.VMEM((lots, 2 * js * (FACTORS + 8), LANES), F32),
+            pltpu.VMEM((lots, js * (FACTORS + 8), LANES), F32),
             pltpu.VMEM(w_exit.shape, F32),
             pltpu.VMEM((FACTORS, LANES, per * depth), BF16),
-            pltpu.VMEM((lots * 2 * js, FACTORS * LANES), BF16),
-            pltpu.VMEM((NY, rows, 2 * js, depth), BF16),
-            pltpu.VMEM((NY, rows, 2 * js, depth), BF16),
+            pltpu.VMEM((lots * js, FACTORS * LANES), BF16),
+            pltpu.VMEM((NC, NY, rows, js, depth), BF16),
+            pltpu.VMEM((NC, NY, rows, js, depth), BF16),
             pltpu.VMEM(pair.shape, F32),
             pltpu.SemaphoreType.DMA((len(later),)),
             pltpu.SemaphoreType.DMA((2 * chunks,)),
         ]
         + sems(wide, wide, NX, NY, NX - 1, NY - 1)
         + sems((chunks, NX - 1), (chunks, wide), (chunks, wide), (chunks, NX - 1))
-        + sems((rows, NY), (rows, NX), (rows, NX), NY - 1),
+        + sems((rows, NY), (rows, NX), (rows, NX), (NC, NY - 1)),
         compiler_params=remote(0),
-    )(pair.reshape(rows * length, depth), w_bias.T, flanks.T, *later)
+    )(*later)
     return aligned.transpose(0, 2, 1, 3).reshape(total, rows, width), pair_after
 
 

time: 87.4 us -> 83.1 us (0.951)
  Pallas kernels: 83.7 us -> 80.8 us
  local copies, waits for them, and re-layouts: 2.89 us -> 1.45 us
    pallas_call x1, Pallas kernels: 83.7 us -> 80.8 us  [shards(): pl.pallas_call(block_kernel, out_shape=(pltpu.VMEM((total, width // LANES...]
    unnamed x4 -> x2, local copies, waits for them, and re-layouts: 2.89 us -> 1.45 us
where the time goes in v5:
time: 83.1 us; the launch traced here: 82.9 us
  Pallas kernels  80.8 us (97%)
  local copies, waits for them, and re-layouts  1.45 us (2%)
    pallas_call x1, Pallas kernels, shards(): pl.pallas_call(block_kernel, out_shape=(pltpu.VMEM((total, width // LANES...  80.8 us

profile of v5, /device:TPU:513, one launch (start us, length us, event | category | flops | bytes accessed | tf_op | source)
XLA Modules:
  0.0 82.9 jit_solution(15112388099597653325)
XLA Ops:
  0.6 80.8 %shard_map.113 = (bf16[512,2,2,128]{3,2,1,0:T(2,128)(2,1)S(1)}, bf16[2,256,128]{2,1,0:T(8,128)(2,1)S(1)}) custom-call(bf16[512,128]{1,0:T(8,128)(2,1)} %bitcast.7, bf16[8,128]{1,0:T(8,128)(2,1)} %bitcast.9, bf16[64,256]{1,0:T(8,128)(2,1)} %bitcast.8, bf16[4,256,256]{2,1,0:T(8,128)(2,1)} %msa_hbm.1, s32[256,256]{1,0:T(8,128)} %drop_hbm.1, ...), custom_call_target="tpu_custom_call" | custom-call | tf_op jit(solution)/shard_map/pallas_call | solution.py:464
  81.5 0.8 copy.14
  82.3 0.7 copy.15

commit v6 on v5

--- a/solution.py
+++ b/solution.py
@@ -193,7 +193,7 @@
         g[s] = nn(m1, w_ref[:, 3 * width : 4 * width])
         return carry
 
-    lax.fori_loop(0, seqs, project, 0)
+    lax.fori_loop(0, seqs, project, 0, unroll=2)
     for m in mine:
         m.wait()
     for m in first0:
@@ -224,18 +224,24 @@
             raw[s, h] = nt(q[s, :, tile] * mask, k[s, :, tile])
         return carry
 
-    lax.fori_loop(0, seqs, score, 0)
+    lax.fori_loop(0, seqs // 2, score, 0, unroll=2)
     other = place(x, y, 1 - c)
     third = []
     onward0 = far(ring_x, x, to_x, lambda n: s2.at[n], lambda n: r2.at[n], second0)
     onward1 = far(ring_y, y, to_y, lambda n: s3.at[n], lambda n: r3.at[n], second1)
-    for d in (2, 6, 1, 7, 3, 5, 4):
-        landed(second0, onward0, d)
-        block = ring_x((x + NX - d) % NX)
-        third.append(push(block, block, s4.at[d - 1], r4.at[d - 1], other))
-        landed(second1, onward1, d)
-        block = ring_y((y + NY - d) % NY)
-        third.append(push(block, block, s5.at[d - 1], r5.at[d - 1], other))
+
+    def hand_bias(ds):
+        for d in ds:
+            landed(second0, onward0, d)
+            block = ring_x((x + NX - d) % NX)
+            third.append(push(block, block, s4.at[d - 1], r4.at[d - 1], other))
+            landed(second1, onward1, d)
+            block = ring_y((y + NY - d) % NY)
+            third.append(push(block, block, s5.at[d - 1], r5.at[d - 1], other))
+
+    hand_bias((2, 6, 1, 7))
+    lax.fori_loop(seqs // 2, seqs, score, 0, unroll=2)
+    hand_bias((3, 5, 4))
     for m in third:
         m.wait_recv()
     for t in range(2):

time: 83.1 us -> 83.2 us (level)
  no operation moved by 1% of the time
where the time goes in v6:
time: 83.2 us; the launch traced here: 83 us
  Pallas kernels  81 us (97%)
  local copies, waits for them, and re-layouts  1.45 us (2%)
    pallas_call x1, Pallas kernels, shards(): pl.pallas_call(block_kernel, out_shape=(pltpu.VMEM((total, width // LANES...  81 us

profile of v6, /device:TPU:513, one launch (start us, length us, event | category | flops | bytes accessed | tf_op | source)
XLA Modules:
  0.0 83.0 jit_solution(10340873946888039807)
XLA Ops:
  0.6 81.0 %shard_map.113 = (bf16[512,2,2,128]{3,2,1,0:T(2,128)(2,1)S(1)}, bf16[2,256,128]{2,1,0:T(8,128)(2,1)S(1)}) custom-call(bf16[512,128]{1,0:T(8,128)(2,1)} %bitcast.7, bf16[8,128]{1,0:T(8,128)(2,1)} %bitcast.9, bf16[64,256]{1,0:T(8,128)(2,1)} %bitcast.8, bf16[4,256,256]{2,1,0:T(8,128)(2,1)} %msa_hbm.1, s32[256,256]{1,0:T(8,128)} %drop_hbm.1, ...), custom_call_target="tpu_custom_call" | custom-call | tf_op jit(solution)/shard_map/pallas_call | solution.py:470
  81.6 0.8 copy.14
  82.4 0.7 copy.15
